TPU v7x, 8 devices: a whole 2x2x1 slice. The times are simulated.
8 devices in a mesh: batch: 1 (over z), gz: 2 (over y), gy: 2 (over x), gx: 2 (over core).
Axes of the slice: x: 2, y: 2, z: 1, core: 2. Of those that a mesh axis runs over, the one named last changes fastest.
Arguments:
- rhs_grid: float32 [256, 256, 256], P(('batch', 'gz'), 'gy', 'gx')
- init_grid: float32 [256, 256, 256], P(('batch', 'gz'), 'gy', 'gx')
- coarse_inv: float32 [512, 512], replicated
Outputs:
- output: float32 [256, 256, 256], P(('batch', 'gz'), 'gy', 'gx')
All inputs are finite; a program needn't handle non-finite values.
Results may differ from a plain program's by a relative error of at most 0.001.
Values sent between devices are 32-bit elements.
A program may use at most 1 GiB of HBM per device.

v0:
```python
import jax
import jax.numpy as jnp
from jax import lax
from jax.sharding import PartitionSpec as P

OMEGA = 2.0 / 3.0
CYCLES = 2
SWEEPS = 2
GRID_AXES = ('gz', 'gy', 'gx')


def solution(mesh):
    axis_lens = tuple(mesh.shape[axis_name] for axis_name in GRID_AXES)
    grid_spec = P(('batch', 'gz'), 'gy', 'gx')

    def with_ghosts(iterate, axis_id):
        extent = iterate.shape[axis_id]
        first_face = lax.slice_in_dim(iterate, 0, 1, axis=axis_id)
        last_face = lax.slice_in_dim(iterate, extent - 1, extent, axis=axis_id)
        axis_name = GRID_AXES[axis_id]
        axis_len = axis_lens[axis_id]
        if axis_len == 1:
            low_ghost = -first_face
            high_ghost = -last_face
        else:
            from_below = lax.ppermute(last_face, axis_name, [(src_id, src_id + 1) for src_id in range(axis_len - 1)])
            from_above = lax.ppermute(first_face, axis_name, [(src_id + 1, src_id) for src_id in range(axis_len - 1)])
            position = lax.axis_index(axis_name)
            low_ghost = jnp.where(position == 0, -first_face, from_below)
            high_ghost = jnp.where(position == axis_len - 1, -last_face, from_above)
        return jnp.concatenate([low_ghost, iterate, high_ghost], axis=axis_id)

    def neighbour_sum(iterate):
        nbr_total = jnp.zeros_like(iterate)
        for axis_id in range(3):
            extent = iterate.shape[axis_id]
            padded = with_ghosts(iterate, axis_id)
            nbr_total = nbr_total + lax.slice_in_dim(padded, 0, extent, axis=axis_id) + lax.slice_in_dim(padded, 2, extent + 2, axis=axis_id)
        return nbr_total

    def jacobi(iterate, source, edge_cells):
        return (1.0 - OMEGA) * iterate + (OMEGA / 6.0) * (source * (1.0 / (edge_cells * edge_cells)) + neighbour_sum(iterate))

    def residual(iterate, source, edge_cells):
        return source - (6.0 * iterate - neighbour_sum(iterate)) * float(edge_cells * edge_cells)

    def restrict(fine_grid):
        dim_z, dim_y, dim_x = fine_grid.shape
        return fine_grid.reshape(dim_z // 2, 2, dim_y // 2, 2, dim_x // 2, 2).mean(axis=(1, 3, 5))

    def prolong(coarse):
        for axis_id in range(3):
            extent = coarse.shape[axis_id]
            padded = with_ghosts(coarse, axis_id)
            low_child = 0.75 * coarse + 0.25 * lax.slice_in_dim(padded, 0, extent, axis=axis_id)
            high_child = 0.75 * coarse + 0.25 * lax.slice_in_dim(padded, 2, extent + 2, axis=axis_id)
            new_shape = list(coarse.shape)
            new_shape[axis_id] = 2 * extent
            coarse = jnp.stack([low_child, high_child], axis=axis_id + 1).reshape(new_shape)
        return coarse

    def coarse_solve(source, coarse_inv):
        gathered = lax.all_gather(source, 'gx', axis=2, tiled=True)
        gathered = lax.all_gather(gathered, 'gy', axis=1, tiled=True)
        gathered = lax.all_gather(gathered, 'gz', axis=0, tiled=True)
        solved = jnp.dot(coarse_inv, gathered.reshape(-1), precision=lax.Precision.HIGHEST).reshape(gathered.shape)
        starts = tuple(lax.axis_index(GRID_AXES[axis_id]) * source.shape[axis_id] for axis_id in range(3))
        return lax.dynamic_slice(solved, starts, source.shape)

    def vcycle(iterate, source, coarse_inv, coarse_edge):
        edge_cells = iterate.shape[0] * axis_lens[0]
        if edge_cells == coarse_edge:
            return coarse_solve(source, coarse_inv)
        for sweep_id in range(SWEEPS):
            iterate = jacobi(iterate, source, edge_cells)
        coarse_rhs = restrict(residual(iterate, source, edge_cells))
        correction = vcycle(jnp.zeros_like(coarse_rhs), coarse_rhs, coarse_inv, coarse_edge)
        iterate = iterate + prolong(correction)
        for sweep_id in range(SWEEPS):
            iterate = jacobi(iterate, source, edge_cells)
        return iterate

    def local_cycles(rhs_grid, init_grid, coarse_inv):
        coarse_edge = int(round(coarse_inv.shape[0] ** (1.0 / 3.0)))
        iterate = init_grid
        for cycle_id in range(CYCLES):
            iterate = vcycle(iterate, rhs_grid, coarse_inv, coarse_edge)
        return iterate

    return jax.shard_map(local_cycles, mesh=mesh, in_specs=(grid_spec, grid_spec, P()), out_specs=grid_spec, check_vma=False)
```

profile of v0, /device:TPU:0, one launch (start us, length us, event | category | flops | bytes accessed | tf_op | source)
XLA Modules:
  0.0 3952.6 jit_solution(12702579876744414164)
XLA Ops:
  7.0 6.4 collective-permute-start.20
  14.7 9.3 copy.589
  24.0 13.2 fusion.575
  45.3 5.2 copy.596
  50.5 9.4 copy.590
  133.8 5.7 collective-permute-start.18
  168.2 16.1 negate_select_fusion.19
  186.7 33.2 fusion.75
  219.8 8.1 fusion.572
  228.3 5.2 copy.607
  264.8 16.1 negate_select_fusion.17
  283.3 33.2 fusion.67
  316.4 8.1 fusion.569
  334.4 5.2 copy.613
  361.0 16.1 negate_select_fusion.15
  379.4 35.3 fusion.59
  414.7 9.3 copy.616
  424.0 538.6 %reshape.130 = f32[64,2,64,2,64,2]{5,4,3,2,1,0:T(8,128)} reshape(f32[128,128,128]{2,1,0:T(8,128)} %copy.616) | data formatting | bytes 16777216 | tf_op jit(solution)/shard_map/reshape | solution.py:49
  962.6 160.9 %reduce_sum.90 = f32[64,64,64]{2,1,0:T(8,128)} reduce(f32[64,2,64,2,64,2]{5,4,3,2,1,0:T(8,128)} %reshape.130, f32[]{:T(128)} %constant.40.clone.1), dimensions={1,3,5}, to_apply=%region_0.1 | reduce | flops 1835008 | bytes 9437188 | tf_op jit(solution)/shard_map/reduce_sum | solution.py:49
  1158.4 9.0 fusion.180
  1201.1 71.4 %reshape.131 = f32[32,2,32,2,32,2]{5,4,3,2,1,0:T(8,128)} reshape(f32[64,64,64]{2,1,0:T(8,128)} %fusion.172) | data formatting | bytes 2097152 | tf_op jit(solution)/shard_map/reshape | solution.py:49
  1272.6 21.8 reduce_sum.91
  1333.0 7.1 reshape.132
  1428.5 7.0 fusion.542
  1785.4 7.8 copy.673
  1800.3 6.4 fusion.97
  1811.0 9.2 copy.674
  1820.3 9.3 copy.675
  1829.6 11.9 add.1380
  1841.5 13.2 fusion.566
  1885.6 16.1 negate_select_fusion.13
  1904.1 33.2 fusion.51
  1937.2 8.1 fusion.563
  1982.0 16.1 negate_select_fusion.11
  2000.5 33.2 fusion.43
  2033.6 8.1 fusion.560
  2078.1 16.1 negate_select_fusion.9
  2096.6 33.2 fusion.35
  2129.7 8.1 fusion.557
  2174.4 16.1 negate_select_fusion.7
  2192.9 33.2 fusion.27
  2226.0 8.1 fusion.554
  2270.4 16.1 negate_select_fusion.5
  2288.8 35.3 fusion.19
  2324.0 9.3 copy.697
  2333.3 538.6 %reshape.151 = f32[64,2,64,2,64,2]{5,4,3,2,1,0:T(8,128)} reshape(f32[128,128,128]{2,1,0:T(8,128)} %copy.697) | data formatting | bytes 16777216 | tf_op jit(solution)/shard_map/reshape | solution.py:49
  2871.9 160.9 %reduce_sum.95 = f32[64,64,64]{2,1,0:T(8,128)} reduce(f32[64,2,64,2,64,2]{5,4,3,2,1,0:T(8,128)} %reshape.151, f32[]{:T(128)} %constant.40.clone.1), dimensions={1,3,5}, to_apply=%region_5.6 | reduce | flops 1835008 | bytes 9437188 | tf_op jit(solution)/shard_map/reduce_sum | solution.py:49
  3066.0 9.0 fusion.142
  3108.9 71.4 %reshape.152 = f32[32,2,32,2,32,2]{5,4,3,2,1,0:T(8,128)} reshape(f32[64,64,64]{2,1,0:T(8,128)} %fusion.134) | data formatting | bytes 2097152 | tf_op jit(solution)/shard_map/reshape | solution.py:49
  3180.3 21.8 reduce_sum.96
  3240.4 7.1 reshape.153
  3335.6 7.0 fusion.540
  3692.3 7.8 copy.763
  3707.2 6.4 fusion.85
  3717.9 9.2 copy.764
  3727.1 9.3 copy.765
  3736.4 11.9 add.1556
  3748.4 13.2 fusion.551
  3792.5 16.1 negate_select_fusion.3
  3811.0 33.2 fusion.11
  3844.1 8.1 fusion.548
  3889.0 16.1 negate_select_fusion.1
  3907.4 35.7 fusion.3
  3943.1 9.2 copy.774
  (1390 shorter events, 1554.8 us)
Async XLA Ops:
  0.0 133.8 %collective-permute-start.23 = (f32[64,64,1]{1,0,2:T(8,128)S(1)}, f32[64,64,1]{1,0,2:T(8,128)S(1)}, u32[]{:S(2)}, u32[]{:S(2)}) collective-permute-start(f32[64,64,1]{1,0,2:T(8,128)S(1)} %broadcast.332), channel_id=1, source_target_pairs={{1,0},{3,2},{5,4},{7,6}} | collective-permute-start | bytes 49160 | tf_op jit(solution)/shard_map/ppermute | solution.py:27
  1.4 140.3 %collective-permute-start.22 = (f32[64,64,1]{1,0,2:T(8,128)S(1)}, f32[64,64,1]{1,0,2:T(8,128)}, u32[]{:S(2)}, u32[]{:S(2)}) collective-permute-start(f32[64,64,1]{1,0,2:T(8,128)S(1)} %broadcast.332), channel_id=1, source_target_pairs={{0,1},{2,3},{4,5},{6,7}} | collective-permute-start | bytes 49160 | tf_op jit(solution)/shard_map/ppermute | solution.py:26
  5.7 140.3 %collective-permute-start.21 = (f32[64,1,64]{2,1,0:T(1,128)}, f32[64,1,64]{2,1,0:T(1,128)}, u32[]{:S(2)}, u32[]{:S(2)}) collective-permute-start(f32[64,1,64]{2,1,0:T(1,128)} %broadcast.330), channel_id=1, source_target_pairs={{2,0},{3,1},{6,4},{7,5}} | collective-permute-start | bytes 49160 | tf_op jit(solution)/shard_map/ppermute | solution.py:27
  7.0 141.7 %collective-permute-start.20 = (f32[64,1,64]{2,1,0:T(1,128)}, f32[64,1,64]{2,1,0:T(1,128)}, u32[]{:S(2)}, u32[]{:S(2)}) collective-permute-start(f32[64,1,64]{2,1,0:T(1,128)} %broadcast.330), channel_id=1, source_target_pairs={{0,2},{1,3},{4,6},{5,7}} | collective-permute-start | bytes 49160 | tf_op jit(solution)/shard_map/ppermute | solution.py:26
  13.4 46.5 %collective-permute-start.77 = (f32[8,8,1]{2,1,0:T(8,128)S(1)}, f32[8,8,1]{2,1,0:T(8,128)S(1)}, u32[]{:S(2)}, u32[]{:S(2)}) collective-permute-start(f32[8,8,1]{2,1,0:T(8,128)S(1)} %broadcast.362), channel_id=1, source_target_pairs={{1,0},{3,2},{5,4},{7,6}} | collective-permute-start | bytes 776 | tf_op jit(solution)/shard_map/ppermute | solution.py:27
  131.9 20.8 collective-permute-start.19
  133.8 21.5 collective-permute-start.18
  145.9 17.6 collective-permute-start.1
  148.6 35.7 collective-permute-start.2
  152.7 31.6 collective-permute-start.3
  155.4 29.9 collective-permute-start.4
  157.3 28.0 collective-permute-start.5
  233.6 20.3 collective-permute-start.6
  245.5 35.5 collective-permute-start.8
  250.1 30.9 collective-permute-start.9
  251.4 30.5 collective-permute-start.10
  253.8 28.0 collective-permute-start.11
  330.2 19.7 collective-permute-start.12
  341.8 35.3 collective-permute-start.14
  346.1 31.0 collective-permute-start.15
  347.4 30.6 collective-permute-start.16
  349.9 28.1 collective-permute-start.17
  1133.1 16.9 collective-permute-start.28
  1139.7 18.5 collective-permute-start.24
  1178.5 18.0 collective-permute-start.30
  1734.6 18.0 collective-permute-start.156
  1870.3 31.5 collective-permute-start.170
  1871.9 29.9 collective-permute-start.171
  1873.2 29.5 collective-permute-start.172
  1874.7 28.0 collective-permute-start.173
  1951.0 20.1 collective-permute-start.174
  1962.7 35.5 collective-permute-start.176
  1967.3 30.9 collective-permute-start.177
  1968.6 30.5 collective-permute-start.178
  1971.1 28.0 collective-permute-start.179
  2047.4 19.7 collective-permute-start.180
  2059.0 35.2 collective-permute-start.182
  2063.3 30.9 collective-permute-start.183
  2064.6 30.6 collective-permute-start.184
  2067.1 28.1 collective-permute-start.185
  2143.5 19.7 collective-permute-start.186
  2155.1 35.4 collective-permute-start.188
  2159.4 31.2 collective-permute-start.189
  2160.7 30.8 collective-permute-start.190
  2163.2 28.3 collective-permute-start.191
  2239.8 19.7 collective-permute-start.192
  2251.4 35.1 collective-permute-start.194
  2255.7 30.8 collective-permute-start.195
  2257.0 30.4 collective-permute-start.196
  2259.5 27.9 collective-permute-start.197
  3040.7 16.9 collective-permute-start.202
  3047.3 18.5 collective-permute-start.198
  3086.2 18.0 collective-permute-start.204
  3641.5 18.0 collective-permute-start.312
  3777.1 31.5 collective-permute-start.326
  3778.7 29.9 collective-permute-start.327
  3780.0 29.5 collective-permute-start.328
  3781.5 28.0 collective-permute-start.329
  3857.9 20.1 collective-permute-start.330
  3867.4 16.9 collective-permute-start.331
  3869.6 35.5 collective-permute-start.332
  3874.2 30.9 collective-permute-start.333
  3875.4 30.6 collective-permute-start.334
  3877.9 28.1 collective-permute-start.335
  (327 other events, 4831.2 us)
where the time goes:
time: 3970 us; the launch traced here: 3950 us
  local copies, waits for them, and re-layouts  1850 us (47%)
  other arithmetic  1130 us (28%)
  starting transfers between devices  761 us (19%)
  waiting for transfers between devices  174 us (4%)
    reshape x10, local copies, waits for them, and re-layouts, restrict(): fine_grid.reshape(dim_z // 2, 2, dim_y // 2, 2, dim_x // 2, 2)  1240 us
    ppermute x168, starting transfers between devices, with_ghosts(): lax.ppermute(last_face, axis_name, [(src_id, src_id + 1) for src_id in ra...  538 us
    reduce_sum x10, other arithmetic, restrict(): fine_grid.reshape(dim_z // 2, 2, dim_y // 2, 2, dim_x // 2, 2)  378 us
    add x32, other arithmetic, jacobi(): (1.0 - OMEGA) * iterate  306 us
    select_n x168, other arithmetic, with_ghosts(): low_ghost = jnp.where(position == 0, -first_face, from_below)  235 us
    ppermute x168, starting transfers between devices, with_ghosts(): lax.ppermute(first_face, axis_name, [(src_id + 1, src_id) for src_id in r...  223 us
    slice x176, local copies, waits for them, and re-layouts, with_ghosts(): last_face = lax.slice_in_dim(iterate, extent - 1, extent, axis=axis_id)  215 us
    ppermute x168, waiting for transfers between devices, with_ghosts(): lax.ppermute(first_face, axis_name, [(src_id + 1, src_id) for src_id in r...  164 us
  transfers between devices with their start and end apart: 336, of which 101 were waited for; matrix products, arithmetic and copies ran while one was open for 13% of the time, Pallas kernels for 0%

commit v1 on v0

v1 whole, which is shorter than its diff:
```python
import jax
import jax.numpy as jnp
from jax import lax
from jax.experimental import pallas as pl
from jax.experimental.pallas import tpu as pltpu
from jax.sharding import PartitionSpec as P

OMEGA = 2.0 / 3.0
C6 = OMEGA / 6.0
CYCLES = 2
MESH = pl.DeviceIdType.MESH
F32 = jnp.float32
SUB, LN = 8, 128
HALO_PLANES = {1: 4, 2: 5}


class Level:
    def __init__(self, idx, n, off, shape, pos, split):
        self.idx, self.n, self.shape = idx, n, shape
        self.oz, self.oy, self.ox = off
        self.split = split
        if split:
            self.lo = tuple(o - p * n for o, p in zip(off, pos))
            self.hi = tuple(l + 2 * n for l in self.lo)
        else:
            self.lo = off
            self.hi = tuple(o + n for o in off)
        wide = SUB if (split and idx > 0) else 0
        self.zs = self.oz - wide * pos[0] if wide else self.oz
        self.ys = self.oy - wide * pos[1] if wide else self.oy
        self.nzb = (n + wide) // SUB
        self.nyt = (n + wide) // SUB
        if split:
            self.ghosts = [(jnp.where(pos[0] == 0, self.oz - 1, self.oz + n), jnp.where(pos[0] == 0, self.oz, self.oz + n - 1))]
        else:
            self.ghosts = [(self.oz - 1, self.oz), (self.oz + n, self.oz + n - 1)]


def solve_kernel(f_hbm, u_hbm, c_hbm, out_hbm,
                 ua, ub, fr, tr, v1a, v1b, b1, v2a, v2b, b2, v3a, v3b, b3, v4a, v4b, b4, e5, b5, cinv,
                 xs, xg, yp, yg, p1s, p1r, p2s, p2r, g3, ssem, rsem, lsem):
    pz, py, px = lax.axis_index('gz'), lax.axis_index('gy'), lax.axis_index('gx')
    pos = (pz, py, px)
    lane = lax.broadcasted_iota(jnp.int32, (SUB, LN), 1)
    row = lax.broadcasted_iota(jnp.int32, (SUB, LN), 0)
    levels = [
        Level(0, LN, (1, SUB, 0), (130, 144), pos, True),
        Level(1, 64, (9, 16, 32), (82, 96), pos, True),
        Level(2, 32, (9, 16, 48), (50, 64), pos, True),
        Level(3, 32, (1, 16, 48), (34, 72), pos, False),
        Level(4, 16, (1, 16, 48), (18, 48), pos, False),
        Level(5, SUB, (1, 16, 48), (10, 32), pos, False),
    ]
    lev0 = levels[0]
    bnd = jnp.where(px == 0, 0, 127)
    recv = 127 - bnd
    sh_in = jnp.where(px == 0, 1, 127)
    sh_out = LN - sh_in

    def dev(code):
        ids = {}
        if code & 4:
            ids['gz'] = 1 - pz
        if code & 2:
            ids['gy'] = 1 - py
        if code & 1:
            ids['gx'] = 1 - px
        return ids

    def remote(src, dst, k, code):
        return pltpu.make_async_remote_copy(src_ref=src, dst_ref=dst, send_sem=ssem.at[k], recv_sem=rsem.at[k],
                                            device_id=dev(code), device_id_type=MESH)

    def loop(n, body):
        lax.fori_loop(0, n, lambda i, c: (body(i), c)[1], 0)

    load_u = pltpu.make_async_copy(u_hbm, ua.at[pl.ds(1, LN), pl.ds(SUB, LN), :], lsem.at[0])
    load_f = pltpu.make_async_copy(f_hbm, fr, lsem.at[1])
    load_c = [pltpu.make_async_copy(c_hbm.at[:, pl.ds(LN * j, LN)], cinv.at[j], lsem.at[2 + j]) for j in range(4)]
    load_u.start()
    load_f.start()
    for copy in load_c:
        copy.start()

    def zero(ref):
        planes, rows = ref.shape[0], ref.shape[1]

        def body(i):
            ref[i] = jnp.zeros((rows, LN), F32)
        loop(planes, body)

    for ref in (v1a, v1b, b1, v2a, v2b, b2, v3a, v3b, b3, v4a, v4b, b4, e5):
        zero(ref)

    def zero_rows(i):
        for ref in (ua, ub):
            ref[i, pl.ds(0, SUB), :] = jnp.zeros((SUB, LN), F32)
            ref[i, pl.ds(136, SUB), :] = jnp.zeros((SUB, LN), F32)
    loop(130, zero_rows)

    barrier = pltpu.get_barrier_semaphore()
    for code in range(1, SUB):
        pl.semaphore_signal(barrier, inc=1, device_id=dev(code), device_id_type=MESH)
    pl.semaphore_wait(barrier, 7)

    def coefs(lev, y0):
        r = row + y0
        inside = (r >= lev.lo[1]) & (r < lev.hi[1]) & (lane >= lev.lo[2]) & (lane < lev.hi[2])
        one, nil = jnp.ones((SUB, LN), F32), jnp.zeros((SUB, LN), F32)
        nb = (jnp.where(r == lev.lo[1], one, nil) + jnp.where(r == lev.hi[1] - 1, one, nil)
              + jnp.where(lane == lev.lo[2], one, nil) + jnp.where(lane == lev.hi[2] - 1, one, nil))
        return inside, nb

    def zghost_tile(lev, ref, y0):
        for ghost, face in lev.ghosts:
            ref[ghost, pl.ds(y0, SUB), :] = -ref[face, pl.ds(y0, SUB), :]

    def zghost(lev, ref):
        loop(lev.shape[1] // SUB, lambda t: zghost_tile(lev, ref, pl.multiple_of(SUB * t, SUB)))

    def plain_sum(src, z0, y0):
        u = src[pl.ds(z0 - 1, 10), pl.ds(y0, SUB), :]
        c = u[1:9]
        s = u[0:SUB] + u[2:10]
        s = s + src[pl.ds(z0, SUB), pl.ds(y0 - 1, SUB), :] + src[pl.ds(z0, SUB), pl.ds(y0 + 1, SUB), :]
        return c, s

    def full_sum(lev, src, z0, y0, ghost):
        c, s = plain_sum(src, z0, y0)
        if lev.idx:
            return c, s + pltpu.roll(c, 1, 2) + pltpu.roll(c, 127, 2)
        k = z0 - 1
        g = jnp.stack([pltpu.roll(ghost, lax.rem(recv + LN - (k + j), LN), 1) for j in range(SUB)])
        inner = pltpu.roll(c, sh_in, 2)
        outer = pltpu.roll(c, sh_out, 2)
        s = s + jnp.where((lane == bnd)[None], 0.0, inner) + jnp.where((lane == recv)[None], g, outer)
        return c, s

    def pack_block(block, k, pk):
        for j in range(SUB):
            pk = jnp.where(lane == k + j, pltpu.roll(block[j], lax.rem(k + j + LN - recv, LN), 1), pk)
        return pk

    def sweep(lev, src, dst, rhs, par=0):
        first = rhs is None

        def ytile(t):
            y0 = pl.multiple_of(lev.ys + SUB * t, SUB)
            inside, nb = coefs(lev, y0)
            cc = (1.0 - OMEGA) - C6 * nb
            if first:
                ca, cb = jnp.where(inside, C6 * (cc + 1.0), 0.0), jnp.where(inside, C6 * C6, 0.0)
            elif lev.idx:
                ca, cb = jnp.where(inside, cc, 0.0), jnp.where(inside, C6, 0.0)
            else:
                ca, cb = cc, C6
            ghost = None if lev.idx else xg[par, pl.ds(pl.multiple_of(SUB * t, SUB), SUB), :]

            def zblk(k, pk):
                z0 = lev.zs + SUB * k
                c, s = full_sum(lev, src, z0, y0, ghost)
                if lev.idx == 0:
                    s = s + fr[pl.ds(SUB * k, SUB), pl.ds(pl.multiple_of(SUB * t, SUB), SUB), :] * (1.0 / 65536.0)
                elif not first:
                    s = s + rhs[pl.ds(z0, SUB), pl.ds(y0, SUB), :]
                new = ca * c + cb * s
                dst[pl.ds(z0, SUB), pl.ds(y0, SUB), :] = new
                return pk if lev.idx else pack_block(new, SUB * k, pk)

            pk = lax.fori_loop(0, lev.nzb, zblk, jnp.zeros((SUB, LN), F32))
            if lev.idx == 0:
                xs[1 - par, pl.ds(pl.multiple_of(SUB * t, SUB), SUB), :] = pk
            zghost_tile(lev, dst, y0)

        loop(lev.nyt, ytile)

    def residual_pass(lev, src, rhs, par=0):
        def ytile(t):
            y0 = pl.multiple_of(lev.oy + SUB * t, SUB)
            t0 = pl.multiple_of(SUB * t, SUB)
            _, nb = coefs(lev, y0)
            dd = 6.0 + nb
            ghost = None if lev.idx else xg[par, pl.ds(t0, SUB), :]

            def zblk(k):
                z0 = lev.oz + SUB * k
                c, s = full_sum(lev, src, z0, y0, ghost)
                if lev.idx == 0:
                    b = fr[pl.ds(SUB * k, SUB), pl.ds(t0, SUB), :] * (1.0 / 65536.0)
                else:
                    b = rhs[pl.ds(z0, SUB), pl.ds(y0, SUB), :]
                r = (b + (s - dd * c)).reshape(4, 2, SUB, LN)
                tr[pl.ds(4 * k, 4), pl.ds(t0, SUB), :] = r[:, 0] + r[:, 1]
            loop(lev.n // SUB, zblk)
        loop(lev.n // SUB, ytile)

    def pair_rows(zc, j):
        s = tr[zc, pl.ds(16 * j, SUB, stride=2), :] + tr[zc, pl.ds(16 * j + 1, SUB, stride=2), :]
        return s + pltpu.roll(s, 127, 1)

    def restrict_to(fine, coarse, dst, pack):
        half = fine.n // 2
        own = (lane >= coarse.ox) & (lane < coarse.ox + half)
        idx = jnp.clip(fine.ox + 2 * (lane - coarse.ox), 0, 127)
        face = jnp.where(px == 0, coarse.ox + half - SUB, coarse.ox)
        group = lane // SUB

        def ytile(j):
            y0 = pl.multiple_of(coarse.oy + SUB * j, SUB)

            def zgrp(q):
                pk = jnp.zeros((SUB, LN), F32)
                for i in range(min(16, half)):
                    zc = 16 * q + i
                    s = jnp.take_along_axis(pair_rows(zc, j), idx, axis=1)
                    s = jnp.where(own, 0.5 * s, 0.0)
                    dst[coarse.oz + zc, pl.ds(y0, SUB), :] = s
                    if pack is not None:
                        pk = jnp.where(group == i, pltpu.roll(s, lax.rem(SUB * i + LN - face, LN), 1), pk)
                if pack is not None:
                    pack[q, pl.ds(pl.multiple_of(SUB * j, SUB), SUB), :] = pk
            loop(max(1, half // 16), zgrp)
        loop(half // SUB, ytile)

    def restrict_packed(fine, me):
        idx = fine.ox + 2 * (lane % 16)
        group = lane // 16
        for j in range(2):
            def zgrp(q):
                pk = jnp.zeros((SUB, LN), F32)
                for i in range(SUB):
                    s = jnp.take_along_axis(pair_rows(SUB * q + i, j), idx, axis=1)
                    pk = jnp.where(group == i, 0.5 * s, pk)
                g3[me, q, pl.ds(SUB * j, SUB), :] = pk
            loop(2, zgrp)

    def prolong_add(fine, coarse, esrc, dst, cbase, pack_par=None):
        back_z = (fine.oz - fine.zs) // 2
        back_y = (fine.oy - fine.ys) // 2
        wide = 0 if fine.nyt * SUB == fine.n else 1
        nct = fine.n // 16 + wide
        cy_s = cbase[1] - 2 * back_y
        fy_s = fine.oy - 4 * back_y
        cz_s = cbase[0] - back_z - 1
        ncz = 4 * fine.nzb + 2
        xf = lane - fine.ox
        half = lax.shift_right_arithmetic(xf, 1)
        odd = xf - 2 * half
        i0 = half + cbase[2]
        i1 = i0 + 2 * odd - 1
        inx = (lane >= fine.lo[2]) & (lane < fine.hi[2])
        edge = (lane == fine.lo[2]) | (lane == fine.hi[2] - 1)
        wx = jnp.where(inx, jnp.where(edge, 0.5, 0.75), 0.0)
        wn = jnp.where(inx, 0.25, 0.0)
        i0 = jnp.clip(i0, 0, 127)
        i1 = jnp.clip(i1, 0, 127)

        def spread(v):
            return wx * jnp.take_along_axis(v, i0, axis=1) + wn * jnp.take_along_axis(v, i1, axis=1)

        def ctile(t):
            cy = pl.multiple_of(cy_s + SUB * t, SUB)
            fy = pl.multiple_of(fy_s + 16 * t, SUB)
            r = row + cy
            iny = (r >= coarse.lo[1]) & (r < coarse.hi[1])
            wny = jnp.where(iny, 0.25, 0.0)
            wde = jnp.where(iny, jnp.where(r == coarse.lo[1], 0.5, 0.75), 0.0)
            wdo = jnp.where(iny, jnp.where(r == coarse.hi[1] - 1, 0.5, 0.75), 0.0)

            def plane(i):
                for q in range(2):
                    z = 2 * i + q
                    e = esrc[cz_s + z, pl.ds(cy, SUB), :]
                    dn = esrc[cz_s + z, pl.ds(cy - 1, SUB), :]
                    up = esrc[cz_s + z, pl.ds(cy + 1, SUB), :]
                    tr[z, pl.ds(fy, SUB, stride=2), :] = spread(wde * e + wny * dn)
                    tr[z, pl.ds(fy + 1, SUB, stride=2), :] = spread(wdo * e + wny * up)
            loop(ncz // 2, plane)
        loop(nct, ctile)

        def ytile(t):
            y0 = pl.multiple_of(fine.ys + SUB * t, SUB)

            def zblk(k, pk):
                z0 = fine.zs + SUB * k
                tb = tr[pl.ds(4 * k, 6), pl.ds(y0, SUB), :]
                mid = 0.75 * tb[1:5]
                add = jnp.stack([mid + 0.25 * tb[0:4], mid + 0.25 * tb[2:6]], axis=1).reshape(SUB, SUB, LN)
                new = dst[pl.ds(z0, SUB), pl.ds(y0, SUB), :] + add
                dst[pl.ds(z0, SUB), pl.ds(y0, SUB), :] = new
                return pk if pack_par is None else pack_block(new, SUB * k, pk)

            pk = lax.fori_loop(0, fine.nzb, zblk, jnp.zeros((SUB, LN), F32))
            if pack_par is not None:
                xs[pack_par, pl.ds(pl.multiple_of(SUB * t, SUB), SUB), :] = pk
            zghost_tile(fine, dst, y0)
        loop(fine.nyt, ytile)

    zface = jnp.where(pz == 0, LN, 1)
    zdst = jnp.where(pz == 0, 0, 129)
    yface = jnp.where(py == 0, 135, SUB)
    yghost = jnp.where(py == 0, 136, 7)

    def exchange0(buf, par):
        cx = remote(xs.at[par], xg.at[par], par, 1)
        cx.start()
        cz = remote(buf.at[zface, pl.ds(SUB, LN), :], buf.at[zdst, pl.ds(SUB, LN), :], 2 + par, 4)
        cz.start()

        def take_rows(i):
            for j in range(SUB):
                yp[par, pl.ds(SUB * i + j, 1), :] = buf[SUB * i + j + 1, pl.ds(yface, 1), :]
        loop(16, take_rows)
        cy = remote(yp.at[par], yg.at[par], 4 + par, 2)
        cy.start()
        cy.wait()

        def put_rows(i):
            for j in range(SUB):
                buf[SUB * i + j + 1, pl.ds(yghost, 1), :] = yg[par, pl.ds(SUB * i + j, 1), :]
        loop(16, put_rows)
        cx.wait()
        cz.wait()

    def exchange_wide(lev, ref, sendp, recvp, k):
        n, h = lev.n, HALO_PLANES[lev.idx]
        cx = remote(sendp, recvp, k, 1)
        cx.start()
        cx.wait()
        halo = jnp.where(px == 0, lev.ox + n, lev.ox - SUB)
        inh = (lane >= halo) & (lane < halo + SUB)

        def ytile(t):
            y0 = pl.multiple_of(lev.oy + SUB * t, SUB)

            def zgrp(q):
                pk = recvp[q, pl.ds(pl.multiple_of(SUB * t, SUB), SUB), :]
                for i in range(16):
                    z = lev.oz + 16 * q + i
                    moved = pltpu.roll(pk, lax.rem(halo + LN - SUB * i, LN), 1)
                    ref[z, pl.ds(y0, SUB), :] = jnp.where(inh, moved, ref[z, pl.ds(y0, SUB), :])
            loop(n // 16, zgrp)
        loop(n // SUB, ytile)
        fy = pl.multiple_of(jnp.where(py == 0, lev.oy + n - SUB, lev.oy), SUB)
        hy = pl.multiple_of(jnp.where(py == 0, lev.oy - SUB, lev.oy + n), SUB)
        fz = jnp.where(pz == 0, lev.oz + n - h, lev.oz)
        hz = jnp.where(pz == 0, lev.oz - h, lev.oz + n)
        copies = [
            remote(ref.at[pl.ds(lev.oz, n), pl.ds(fy, SUB), :], ref.at[pl.ds(lev.oz, n), pl.ds(hy, SUB), :], k + 1, 2),
            remote(ref.at[pl.ds(fz, h), pl.ds(lev.oy, n), :], ref.at[pl.ds(hz, h), pl.ds(lev.oy, n), :], k + 2, 4),
            remote(ref.at[pl.ds(fz, h), pl.ds(fy, SUB), :], ref.at[pl.ds(hz, h), pl.ds(hy, SUB), :], k + 3, 6),
        ]
        for c in copies:
            c.start()
        for c in copies:
            c.wait()
        zghost(lev, ref)

    me = 4 * pz + 2 * py + px

    def gather3():
        copies = [remote(g3.at[me], g3.at[me], 14 + code, code) for code in range(1, SUB)]
        for c in copies:
            c.start()
        for c in copies:
            c.wait()
        lev = levels[3]

        def ytile(t):
            y0 = pl.multiple_of(lev.oy + SUB * t, SUB)
            by = t // 2
            r0 = pl.multiple_of(SUB * (t % 2), SUB)

            def zgrp(q):
                bz = q // 2
                total = None
                lo = g3[4 * bz + 2 * by, q % 2, pl.ds(r0, SUB), :]
                hi = g3[4 * bz + 2 * by + 1, q % 2, pl.ds(r0, SUB), :]
                for i in range(SUB):
                    a = pltpu.roll(lo, (lev.ox - 16 * i) % LN, 1)
                    b = pltpu.roll(hi, (lev.ox + 16 - 16 * i) % LN, 1)
                    v = jnp.where((lane >= lev.ox) & (lane < lev.ox + 16), a,
                                  jnp.where((lane >= lev.ox + 16) & (lane < lev.ox + 32), b, 0.0))
                    b3[lev.oz + SUB * q + i, pl.ds(y0, SUB), :] = v
            loop(4, zgrp)
        loop(4, ytile)
        zghost(lev, b3)

    def coarse_solve():
        lev = levels[5]

        def zstep(z, acc):
            b = b5[lev.oz + z, pl.ds(lev.oy, SUB), :] * 64.0
            acc = list(acc)
            for x in range(SUB):
                col = jnp.broadcast_to(b[:, lev.ox + x:lev.ox + x + 1], (SUB, LN))
                for j in range(4):
                    acc[j] = acc[j] + cinv[j, pl.ds(z * 64 + x, SUB, stride=SUB), :] * col
            return tuple(acc)
        acc = lax.fori_loop(0, SUB, zstep, (jnp.zeros((SUB, LN), F32),) * 4)
        lines = [jnp.broadcast_to(jnp.sum(a, axis=0, keepdims=True), (SUB, LN)) for a in acc]
        own = (lane >= lev.ox) & (lane < lev.ox + SUB)
        for z in range(SUB):
            idx = jnp.clip((z % 2) * 64 + row * SUB + lane - lev.ox, 0, 127)
            e5[lev.oz + z, pl.ds(lev.oy, SUB), :] = jnp.where(own, jnp.take_along_axis(lines[z // 2], idx, axis=1), 0.0)
        zghost(lev, e5)

    def base_of(lev):
        return (lev.oz, lev.oy, lev.ox)

    def local_visit(fine, va, vb, rhs, descend, ecoarse, coarse, cbase):
        sweep(fine, rhs, va, None)
        zghost(fine, va)
        residual_pass(fine, va, rhs)
        descend()
        prolong_add(fine, coarse, ecoarse, va, cbase)
        sweep(fine, va, vb, rhs)
        sweep(fine, vb, va, rhs)

    def descend4():
        restrict_to(levels[4], levels[5], b5, None)
        coarse_solve()

    def descend3():
        restrict_to(levels[3], levels[4], b4, None)
        zghost(levels[4], b4)
        local_visit(levels[4], v4a, v4b, b4, descend4, e5, levels[5], base_of(levels[5]))

    def descend2():
        restrict_packed(levels[2], me)
        gather3()
        local_visit(levels[3], v3a, v3b, b3, descend3, v4a, levels[4], base_of(levels[4]))

    def descend1():
        restrict_to(levels[1], levels[2], b2, p2s)
        exchange_wide(levels[2], b2, p2s, p2r, 10)
        oz, oy, ox = base_of(levels[3])
        local_visit(levels[2], v2a, v2b, b2, descend2, v3a, levels[3], (oz + 16 * pz, oy + 16 * py, ox + 16 * px))

    def pack_initial(t):
        y0 = pl.multiple_of(SUB + SUB * t, SUB)
        pk = lax.fori_loop(0, 16, lambda k, pk: pack_block(ua[pl.ds(1 + SUB * k, SUB), pl.ds(y0, SUB), :], SUB * k, pk),
                           jnp.zeros((SUB, LN), F32))
        xs[0, pl.ds(pl.multiple_of(SUB * t, SUB), SUB), :] = pk
        zghost_tile(lev0, ua, y0)

    load_u.wait()
    loop(16, pack_initial)
    load_f.wait()
    for copy in load_c:
        copy.wait()

    def cycle(_):
        exchange0(ua, 0)
        sweep(lev0, ua, ub, fr, 0)
        exchange0(ub, 1)
        sweep(lev0, ub, ua, fr, 1)
        exchange0(ua, 0)
        residual_pass(lev0, ua, fr, 0)
        restrict_to(lev0, levels[1], b1, p1s)
        exchange_wide(levels[1], b1, p1s, p1r, 6)
        local_visit(levels[1], v1a, v1b, b1, descend1, v2a, levels[2], base_of(levels[2]))
        prolong_add(lev0, levels[1], v1a, ua, base_of(levels[1]), 0)
        exchange0(ua, 0)
        sweep(lev0, ua, ub, fr, 0)
        exchange0(ub, 1)
        sweep(lev0, ub, ua, fr, 1)

    loop(CYCLES, cycle)

    store = pltpu.make_async_copy(ua.at[pl.ds(1, LN), pl.ds(SUB, LN), :], out_hbm, lsem.at[0])
    store.start()
    store.wait()


def solution(mesh):
    grid_spec = P(('batch', 'gz'), 'gy', 'gx')

    def vmem(*shape):
        return pltpu.VMEM(shape, F32)

    scratch = [vmem(130, 144, LN), vmem(130, 144, LN), vmem(LN, LN, LN), vmem(66, 144, LN)]
    for shape in ((82, 96), (50, 64), (34, 72), (18, 48)):
        scratch += [vmem(*shape, LN)] * 3
    scratch += [vmem(10, 32, LN), vmem(10, 32, LN), vmem(4, 512, LN)]
    scratch += [vmem(2, LN, LN)] * 4
    scratch += [vmem(4, 64, LN)] * 2 + [vmem(2, 32, LN)] * 2 + [vmem(SUB, 2, 16, LN)]
    scratch += [pltpu.SemaphoreType.DMA((22,)), pltpu.SemaphoreType.DMA((22,)), pltpu.SemaphoreType.DMA((6,))]

    call = pl.pallas_call(
        solve_kernel,
        out_shape=jax.ShapeDtypeStruct((LN, LN, LN), F32),
        in_specs=[pl.BlockSpec(memory_space=pl.ANY)] * 3,
        out_specs=pl.BlockSpec(memory_space=pl.ANY),
        scratch_shapes=scratch,
        name='multigrid',
        compiler_params=pltpu.CompilerParams(collective_id=0, has_side_effects=True, vmem_limit_bytes=67043328),
    )
    return jax.shard_map(call, mesh=mesh, in_specs=(grid_spec, grid_spec, P()), out_specs=grid_spec, check_vma=False)
```

time: 3970 us -> 745 us (0.19)
  local copies, waits for them, and re-layouts: 1850 us -> 7.89 us
  other arithmetic: 1130 us -> 0 us
  starting transfers between devices: 761 us -> 0 us
  Pallas kernels: 0 us -> 737 us
  waiting for transfers between devices: 174 us -> 0 us
    reshape x23 -> x0, local copies, waits for them, and re-layouts: 1270 us -> none  [the longest x10 1240 us: restrict(): fine_grid.reshape(dim_z // 2, 2, dim_y // 2, 2, dim_x // 2, 2)]
    ppermute x336 -> x0, starting transfers between devices: 761 us -> none  [the longest x168 538 us: with_ghosts(): lax.ppermute(last_face, axis_name, [(src_id, src_id + 1) for src_id in ra...]
    pallas_call x0 -> x1, Pallas kernels: none -> 737 us
    reduce_sum x10 -> x0, other arithmetic: 378 us -> none  [restrict(): fine_grid.reshape(dim_z // 2, 2, dim_y // 2, 2, dim_x // 2, 2)]
    add x44 -> x0, other arithmetic: 337 us -> none  [the longest x32 306 us: jacobi(): (1.0 - OMEGA) * iterate]
    slice x196 -> x0, local copies, waits for them, and re-layouts: 285 us -> none  [the longest x176 215 us: with_ghosts(): last_face = lax.slice_in_dim(iterate, extent - 1, extent, axis=axis_id)]
    select_n x188 -> x0, other arithmetic: 261 us -> none  [the longest x168 235 us: with_ghosts(): low_ghost = jnp.where(position == 0, -first_face, from_below)]
    ppermute x336 -> x0, waiting for transfers between devices: 174 us -> none  [the longest x168 164 us: with_ghosts(): lax.ppermute(first_face, axis_name, [(src_id + 1, src_id) for src_id in r...]
  transfers between devices with their start and end apart: 336 -> 0, of which waited for: 101 -> 0; matrix products, arithmetic and copies ran while one was open for 13% -> 0% of each run, Pallas kernels for 0% -> 0%
where the time goes in v1:
time: 745 us
  Pallas kernels  737 us (99%)
  local copies, waits for them, and re-layouts  7.89 us (1%)
    pallas_call x1, Pallas kernels  737 us

profile of v1, /device:TPU:0, one launch (start us, length us, event | category | flops | bytes accessed | tf_op | source)
XLA Modules:
  0.0 744.9 jit_solution(10516873507667653673)
XLA Ops:
  0.0 737.0 %multigrid.1 = f32[128,128,128]{2,1,0:T(8,128)} custom-call(f32[128,128,128]{2,1,0:T(8,128)} %f_hbm.1, f32[128,128,128]{2,1,0:T(8,128)} %u_hbm.1, f32[512,512]{1,0:T(8,128)} %c_hbm.1), custom_call_target="tpu_custom_call" | custom-call | tf_op jit(solution)/shard_map/multigrid/pallas_call
  737.0 7.9 %copy.5 = f32[128,128,128]{2,1,0:T(8,128)} copy(f32[128,128,128]{2,1,0:T(8,128)} %multigrid.1) | data formatting | bytes 16777216

commit v2 on v1

v2 whole, which is shorter than its diff:
```python
import jax
import jax.numpy as jnp
from jax import lax
from jax.experimental import pallas as pl
from jax.experimental.pallas import tpu as pltpu
from jax.sharding import PartitionSpec as P

OMEGA = 2.0 / 3.0
C6 = OMEGA / 6.0
CYCLES = 2
MESH = pl.DeviceIdType.MESH
F32 = jnp.float32
SUB, GRP, LN = 8, 16, 128
HALO_PLANES = {1: 4, 2: 5}
BACK = LN - 1
INV_G2 = 1.0 / 65536.0


class Level:
    def __init__(self, idx, n, off, shape, pos, split):
        self.idx, self.n, self.shape = idx, n, shape
        self.oz, self.oy, self.ox = off
        self.split = split
        if split:
            self.lo = tuple(o - p * n for o, p in zip(off, pos))
            self.hi = tuple(l + 2 * n for l in self.lo)
        else:
            self.lo = off
            self.hi = tuple(o + n for o in off)
        wide = SUB if (split and idx > 0) else 0
        self.zs = self.oz - wide * pos[0] if wide else self.oz
        self.ys = self.oy - wide * pos[1] if wide else self.oy
        self.nzb = (n + wide) // SUB
        self.nyt = (n + wide) // SUB
        if split:
            self.ghosts = [(jnp.where(pos[0] == 0, self.oz - 1, self.oz + n), jnp.where(pos[0] == 0, self.oz, self.oz + n - 1))]
        else:
            self.ghosts = [(self.oz - 1, self.oz), (self.oz + n, self.oz + n - 1)]


def solve_kernel(f_hbm, u_hbm, c_hbm, out_hbm,
                 ua, ub, fr, tr, xr, sx, v1, b1, v2, b2, v3, b3, v4, b4, e5, b5, cinv,
                 xs, xg, yp, yg, p1s, p1r, p2s, p2r, g3, ssem, rsem, lsem):
    pz, py, px = lax.axis_index('gz'), lax.axis_index('gy'), lax.axis_index('gx')
    pos = (pz, py, px)
    lane = lax.broadcasted_iota(jnp.int32, (SUB, LN), 1)
    row = lax.broadcasted_iota(jnp.int32, (SUB, LN), 0)
    nil = jnp.zeros((SUB, LN), F32)
    levels = [
        Level(0, LN, (1, SUB, 0), (130, 144), pos, True),
        Level(1, 64, (9, GRP, 32), (82, 96), pos, True),
        Level(2, 32, (9, GRP, 48), (50, 64), pos, True),
        Level(3, 32, (1, GRP, 48), (34, 72), pos, False),
        Level(4, GRP, (1, GRP, 48), (18, 48), pos, False),
        Level(5, SUB, (1, GRP, 48), (10, 32), pos, False),
    ]
    lev0 = levels[0]
    low_x = px == 0
    face_lane = jnp.where(low_x, (lane + 1) & BACK, lane)
    out_lane = jnp.where(low_x, lane, (lane + 1) & BACK)

    def dev(code):
        ids = {}
        if code & 4:
            ids['gz'] = 1 - pz
        if code & 2:
            ids['gy'] = 1 - py
        if code & 1:
            ids['gx'] = 1 - px
        return ids

    def remote(src, dst, k, code):
        return pltpu.make_async_remote_copy(src_ref=src, dst_ref=dst, send_sem=ssem.at[k], recv_sem=rsem.at[k],
                                            device_id=dev(code), device_id_type=MESH)

    def loop(n, body):
        lax.fori_loop(0, n, lambda i, c: (body(i), c)[1], 0)

    def tile(i):
        return pl.multiple_of(SUB * i, SUB)

    def load(t):
        rows = pl.ds(tile(t), SUB)
        return (pltpu.make_async_copy(u_hbm.at[:, rows, :], ua.at[pl.ds(1, LN), pl.ds(tile(t + 1), SUB), :], lsem.at[t]),
                pltpu.make_async_copy(f_hbm.at[:, rows, :], fr.at[:, rows, :], lsem.at[GRP + t]))

    def start_load(t):
        for copy in load(t):
            copy.start()
    loop(GRP, start_load)
    load_c = [pltpu.make_async_copy(c_hbm.at[:, pl.ds(LN * j, LN)], cinv.at[j], lsem.at[32 + j]) for j in range(4)]
    for copy in load_c:
        copy.start()

    def zero(ref):
        def body(i):
            ref[i] = jnp.zeros(ref.shape[1:], F32)
        loop(ref.shape[0], body)

    for ref in (v1.at[0], v1.at[1], b1, v2.at[0], v2.at[1], b2, v3.at[0], v3.at[1], b3, v4.at[0], v4.at[1], b4, e5):
        zero(ref)

    def zero_rows(i):
        for buf in (ua, ub):
            buf[i, pl.ds(0, SUB), :] = nil
            buf[i, pl.ds(136, SUB), :] = nil
    loop(130, zero_rows)
    zout = jnp.where(pz == 0, 0, 129)

    def zero_plane(t):
        for buf in (ua, ub):
            buf[zout, pl.ds(tile(t), SUB), :] = nil
    loop(18, zero_plane)

    barrier = pltpu.get_barrier_semaphore()
    for code in range(1, SUB):
        pl.semaphore_signal(barrier, inc=1, device_id=dev(code), device_id_type=MESH)
    pl.semaphore_wait(barrier, 7)

    def coefs(lev, y0):
        r = row + y0
        inside = (r >= lev.lo[1]) & (r < lev.hi[1]) & (lane >= lev.lo[2]) & (lane < lev.hi[2])
        one = jnp.ones((SUB, LN), F32)
        nb = (jnp.where(r == lev.lo[1], one, nil) + jnp.where(r == lev.hi[1] - 1, one, nil)
              + jnp.where(lane == lev.lo[2], one, nil) + jnp.where(lane == lev.hi[2] - 1, one, nil))
        return inside, nb

    def zghost_tile(lev, ref, y0):
        for ghost, face in lev.ghosts:
            ref[ghost, pl.ds(y0, SUB), :] = -ref[face, pl.ds(y0, SUB), :]

    def zghost(lev, ref):
        loop(lev.shape[1] // SUB, lambda t: zghost_tile(lev, ref, tile(t)))

    def blocks(count, per, body):
        def step(i):
            for k in range(per):
                body(i * per + k)
        loop(count // per, step)

    def roll_sums(src, zs, nzb, y0):
        for z in range(SUB * nzb):
            c = src[zs + z, pl.ds(y0, SUB), :]
            sx[z] = pltpu.roll(c, 1, 1) + pltpu.roll(c, BACK, 1)

    def stencil(src, zs, k, y0):
        z0 = zs + SUB * k
        v = src[pl.ds(z0 - 1, SUB + 2), pl.ds(y0, SUB), :]
        s = v[0:SUB] + v[2:SUB + 2]
        s = s + src[pl.ds(z0, SUB), pl.ds(y0 - 1, SUB), :] + src[pl.ds(z0, SUB), pl.ds(y0 + 1, SUB), :]
        return v[1:SUB + 1], s + sx[pl.ds(SUB * k, SUB)]

    def sweep(lev, src, dst, rhs):
        first = rhs is None

        def ytile(t):
            y0 = pl.multiple_of(lev.ys + SUB * t, SUB)
            inside, nb = coefs(lev, y0)
            cc = (1.0 - OMEGA) - C6 * nb
            if first:
                ca, cb = jnp.where(inside, C6 * (cc + 1.0), 0.0), jnp.where(inside, C6 * C6, 0.0)
            else:
                ca, cb = jnp.where(inside, cc, 0.0), jnp.where(inside, C6, 0.0)
            roll_sums(src, lev.zs, lev.nzb, y0)

            def block(k):
                c, s = stencil(src, lev.zs, k, y0)
                z0 = lev.zs + SUB * k
                if not first:
                    s = s + rhs[pl.ds(z0, SUB), pl.ds(y0, SUB), :]
                dst[pl.ds(z0, SUB), pl.ds(y0, SUB), :] = ca * c + cb * s
            blocks(lev.nzb, 3 if lev.nzb == 9 else 2 if lev.nzb == 4 else 1, block)
            zghost_tile(lev, dst, y0)
        loop(lev.nyt, ytile)

    def residual_pass(lev, src, rhs):
        def ytile(t):
            y0 = pl.multiple_of(lev.oy + SUB * t, SUB)
            _, nb = coefs(lev, y0)
            dd = 6.0 + nb
            roll_sums(src, lev.oz, lev.n // SUB, y0)

            def block(k):
                c, s = stencil(src, lev.oz, k, y0)
                r = (rhs[pl.ds(lev.oz + SUB * k, SUB), pl.ds(y0, SUB), :] + (s - dd * c)).reshape(4, 2, SUB, LN)
                tr[pl.ds(4 * k, 4), pl.ds(tile(t), SUB), :] = r[:, 0] + r[:, 1]
            blocks(lev.n // SUB, max(1, lev.n // GRP // 2), block)
        loop(lev.n // SUB, ytile)

    def roll_sums0(src, par, t):
        rows = pl.ds(tile(t + 1), SUB)
        ghost = xg[par, pl.ds(tile(t), SUB), :]
        left = jnp.where(low_x, 0.0, ghost)
        right = jnp.where(low_x, ghost, 0.0)
        zlow = jnp.where(pz == 0, 1.0, 0.0)
        below, here = src[0, rows, :], src[1, rows, :]
        for z in range(LN):
            above = src[z + 2, rows, :]
            a = jnp.where(lane == (z - 1) % LN, left, here) + below
            b = jnp.where(lane == z, right, here) + above
            s = pltpu.roll(a, 1, 1) + pltpu.roll(b, BACK, 1) - jnp.where(out_lane == z, here, 0.0)
            if z == 0:
                s = s - zlow * here
            if z == LN - 1:
                s = s - (1.0 - zlow) * here
            sx[z] = s
            below, here = here, above

    def cells0(src, t, z):
        y0, planes = tile(t + 1), pl.ds(z + 1, GRP)
        s = sx[pl.ds(z, GRP)] + src[planes, pl.ds(y0 - 1, SUB), :] + src[planes, pl.ds(y0 + 1, SUB), :]
        return src[planes, pl.ds(y0, SUB), :], s + fr[pl.ds(z, GRP), pl.ds(tile(t), SUB), :]

    def yedge(t):
        r = row + tile(t + 1)
        return jnp.where((r == lev0.lo[1]) | (r == lev0.hi[1] - 1), 1.0, 0.0)

    def sweep0(src, dst, par):
        def ytile(t):
            roll_sums0(src, par, t)
            cc = (1.0 - OMEGA) - C6 * yedge(t)

            def block(k, pk):
                c, s = cells0(src, t, GRP * k)
                new = cc * c + C6 * s
                dst[pl.ds(GRP * k + 1, GRP), pl.ds(tile(t + 1), SUB), :] = new
                for j in range(GRP):
                    pk = jnp.where(face_lane == GRP * k + j, new[j], pk)
                return pk
            xs[1 - par, pl.ds(tile(t), SUB), :] = lax.fori_loop(0, SUB, block, nil)
        loop(GRP, ytile)

    def residual0():
        def ytile(t):
            roll_sums0(ua, 0, t)
            dd = 6.0 + yedge(t)

            def block(k):
                c, s = cells0(ua, t, GRP * k)
                ub[pl.ds(GRP * k + 1, GRP), pl.ds(tile(t + 1), SUB), :] = s - dd * c
            loop(SUB, block)
        loop(GRP, ytile)

    def pair_sums(fine, j):
        for zc in range(fine.n // 2):
            lo, hi = pl.ds(GRP * j, SUB, stride=2), pl.ds(GRP * j + 1, SUB, stride=2)
            if fine.idx:
                s = tr[zc, lo, :] + tr[zc, hi, :]
                sx[zc] = 0.5 * (s + pltpu.roll(s, BACK, 1))
                continue
            lo, hi = pl.ds(GRP * j + SUB, SUB, stride=2), pl.ds(GRP * j + SUB + 1, SUB, stride=2)
            e = ub[2 * zc + 1, lo, :] + ub[2 * zc + 1, hi, :]
            o = ub[2 * zc + 2, lo, :] + ub[2 * zc + 2, hi, :]
            s = pltpu.roll(e, -2 * zc % LN, 1) + pltpu.roll(e + o, (-2 * zc - 1) % LN, 1)
            sx[zc] = 0.5 * (s + pltpu.roll(o, (-2 * zc - 2) % LN, 1))

    def restrict_to(fine, coarse, dst, pack):
        half = fine.n // 2
        own = (lane >= coarse.ox) & (lane < coarse.ox + half)
        idx = (fine.ox + 2 * (lane - coarse.ox)) & BACK
        pidx = fine.ox + 2 * (jnp.where(low_x, half - SUB, 0) + lane % SUB)
        group = lane // SUB
        step = min(GRP, half // 2)

        def ytile(j):
            rows = pl.ds(pl.multiple_of(coarse.oy + SUB * j, SUB), SUB)
            pair_sums(fine, j)

            def move(q):
                for i in range(step):
                    z = step * q + i
                    dst[coarse.oz + z, rows, :] = jnp.where(own, jnp.take_along_axis(sx[z], idx, axis=1), 0.0)
            loop(half // step, move)

            def collect(q):
                pk = nil
                for i in range(GRP):
                    pk = jnp.where(group == i, jnp.take_along_axis(sx[GRP * q + i], pidx, axis=1), pk)
                pack[q, pl.ds(tile(j), SUB), :] = pk
            if pack is not None:
                loop(half // GRP, collect)
        loop(half // SUB, ytile)

    def restrict_packed(fine, me):
        idx = fine.ox + 2 * (lane % GRP)
        group = lane // GRP

        def ytile(j):
            pair_sums(fine, j)

            def collect(q):
                pk = nil
                for i in range(SUB):
                    pk = jnp.where(group == i, jnp.take_along_axis(sx[SUB * q + i], idx, axis=1), pk)
                g3[me, q, pl.ds(tile(j), SUB), :] = pk
            loop(2, collect)
        loop(2, ytile)

    def prolong_add(fine, coarse, esrc, dst, cbase):
        back_z = (fine.oz - fine.zs) // 2
        back_y = (fine.oy - fine.ys) // 2
        nct = fine.n // GRP + (0 if fine.nyt * SUB == fine.n else 1)
        cy_s = cbase[1] - 2 * back_y
        fy_s = fine.oy - 4 * back_y
        cz_s = cbase[0] - back_z - 1
        ncz = 4 * fine.nzb + 2
        xf = lane - fine.ox
        half = lax.shift_right_arithmetic(xf, 1)
        odd = xf - 2 * half
        i0 = half + cbase[2]
        i1 = jnp.clip(i0 + 2 * odd - 1, 0, BACK)
        i0 = jnp.clip(i0, 0, BACK)
        inx = (lane >= fine.lo[2]) & (lane < fine.hi[2])
        edge = (lane == fine.lo[2]) | (lane == fine.hi[2] - 1)
        wx = jnp.where(inx, jnp.where(edge, 0.5, 0.75), 0.0)
        wn = jnp.where(inx, 0.25, 0.0)

        def spread(z):
            for t in range(nct + 2):
                v = esrc[cz_s + z, pl.ds(pl.multiple_of(cy_s + SUB * (t - 1), SUB), SUB), :]
                xr[z, pl.ds(SUB * t, SUB), :] = (wx * jnp.take_along_axis(v, i0, axis=1)
                                                 + wn * jnp.take_along_axis(v, i1, axis=1))

        def spread_two(z):
            spread(2 * z)
            spread(2 * z + 1)
        loop(ncz // 2, spread_two)

        def ctile(t):
            fy = pl.multiple_of(fy_s + GRP * t, SUB)
            r = row + (cy_s + SUB * t)
            iny = (r >= coarse.lo[1]) & (r < coarse.hi[1])
            wny = jnp.where(iny, 0.25, 0.0)
            wde = jnp.where(iny, jnp.where(r == coarse.lo[1], 0.5, 0.75), 0.0)
            wdo = jnp.where(iny, jnp.where(r == coarse.hi[1] - 1, 0.5, 0.75), 0.0)

            def plane(i):
                for q in range(2):
                    z = 2 * i + q
                    e = xr[z, pl.ds(tile(t + 1), SUB), :]
                    tr[z, pl.ds(fy, SUB, stride=2), :] = wde * e + wny * xr[z, pl.ds(tile(t + 1) - 1, SUB), :]
                    tr[z, pl.ds(fy + 1, SUB, stride=2), :] = wdo * e + wny * xr[z, pl.ds(tile(t + 1) + 1, SUB), :]
            loop(ncz // 2, plane)
        loop(nct, ctile)

        def ytile(t):
            y0 = pl.multiple_of(fine.ys + SUB * t, SUB)
            rows = pl.ds(y0, SUB)
            pk = nil
            for k in range(fine.nzb):
                z0 = fine.zs + SUB * k
                tb = tr[pl.ds(4 * k, 6), rows, :]
                mid = 0.75 * tb[1:5]
                add = jnp.stack([mid + 0.25 * tb[0:4], mid + 0.25 * tb[2:6]], axis=1).reshape(SUB, SUB, LN)
                if fine.idx:
                    dst[pl.ds(z0, SUB), rows, :] = dst[pl.ds(z0, SUB), rows, :] + add
                    continue
                for j in range(SUB):
                    z = SUB * k + j
                    new = dst[1 + z, rows, :] + pltpu.roll(add[j], z, 1)
                    dst[1 + z, rows, :] = new
                    pk = jnp.where(face_lane == z, new, pk)
            if fine.idx:
                zghost_tile(fine, dst, y0)
            else:
                xs[0, pl.ds(tile(t), SUB), :] = pk
        loop(fine.nyt, ytile)

    zface = jnp.where(pz == 0, LN, 1)
    zdst = LN + 1 - zface + jnp.where(pz == 0, -1, 1)
    yface = jnp.where(py == 0, 135, SUB)
    yghost = jnp.where(py == 0, 136, 7)

    def exchange0(buf, par):
        cx = remote(xs.at[par], xg.at[par], par, 1)
        cx.start()
        cz = remote(buf.at[zface, pl.ds(SUB, LN), :], buf.at[zdst, pl.ds(SUB, LN), :], 2 + par, 4)
        cz.start()

        def take_rows(i):
            for j in range(SUB):
                yp[par, pl.ds(SUB * i + j, 1), :] = buf[SUB * i + j + 1, pl.ds(yface, 1), :]
        loop(GRP, take_rows)
        cy = remote(yp.at[par], yg.at[par], 4 + par, 2)
        cy.start()
        cy.wait()

        def put_rows(i):
            for j in range(SUB):
                buf[SUB * i + j + 1, pl.ds(yghost, 1), :] = yg[par, pl.ds(SUB * i + j, 1), :]
        loop(GRP, put_rows)
        cx.wait()
        cz.wait()

    def exchange_wide(lev, ref, sendp, recvp, k):
        n, h = lev.n, HALO_PLANES[lev.idx]
        cx = remote(sendp, recvp, k, 1)
        cx.start()
        cx.wait()
        halo = jnp.where(low_x, lev.ox + n, lev.ox - SUB)
        inh = (lane >= halo) & (lane < halo + SUB)

        def ytile(t):
            rows = pl.ds(pl.multiple_of(lev.oy + SUB * t, SUB), SUB)
            for q in range(n // GRP):
                pk = recvp[q, pl.ds(tile(t), SUB), :]
                pk = pltpu.roll(pk, halo, 1)
                for i in range(GRP):
                    z = lev.oz + GRP * q + i
                    ref[z, rows, :] = jnp.where(inh, pltpu.roll(pk, (-SUB * i) % LN, 1), ref[z, rows, :])
        loop(n // SUB, ytile)
        fy = pl.multiple_of(jnp.where(py == 0, lev.oy + n - SUB, lev.oy), SUB)
        hy = pl.multiple_of(jnp.where(py == 0, lev.oy - SUB, lev.oy + n), SUB)
        fz = jnp.where(pz == 0, lev.oz + n - h, lev.oz)
        hz = jnp.where(pz == 0, lev.oz - h, lev.oz + n)
        copies = [
            remote(ref.at[pl.ds(lev.oz, n), pl.ds(fy, SUB), :], ref.at[pl.ds(lev.oz, n), pl.ds(hy, SUB), :], k + 1, 2),
            remote(ref.at[pl.ds(fz, h), pl.ds(lev.oy, n), :], ref.at[pl.ds(hz, h), pl.ds(lev.oy, n), :], k + 2, 4),
            remote(ref.at[pl.ds(fz, h), pl.ds(fy, SUB), :], ref.at[pl.ds(hz, h), pl.ds(hy, SUB), :], k + 3, 6),
        ]
        for c in copies:
            c.start()
        for c in copies:
            c.wait()
        zghost(lev, ref)

    me = 4 * pz + 2 * py + px

    def gather3():
        copies = [remote(g3.at[me], g3.at[me], 14 + code, code) for code in range(1, SUB)]
        for c in copies:
            c.start()
        for c in copies:
            c.wait()
        lev = levels[3]
        in_lo = (lane >= lev.ox) & (lane < lev.ox + GRP)
        in_hi = (lane >= lev.ox + GRP) & (lane < lev.ox + 32)

        def ytile(t):
            rows = pl.ds(pl.multiple_of(lev.oy + SUB * t, SUB), SUB)
            by = t // 2
            r0 = pl.ds(tile(t % 2), SUB)
            for q in range(4):
                lo = g3[4 * (q // 2) + 2 * by, q % 2, r0, :]
                hi = g3[4 * (q // 2) + 2 * by + 1, q % 2, r0, :]
                for i in range(SUB):
                    a = pltpu.roll(lo, (lev.ox - GRP * i) % LN, 1)
                    b = pltpu.roll(hi, (lev.ox + GRP - GRP * i) % LN, 1)
                    b3[lev.oz + SUB * q + i, rows, :] = jnp.where(in_lo, a, jnp.where(in_hi, b, 0.0))
        loop(4, ytile)
        zghost(lev, b3)

    def coarse_solve():
        lev = levels[5]

        def zstep(z, acc):
            b = b5[lev.oz + z, pl.ds(lev.oy, SUB), :] * 64.0
            acc = list(acc)
            for x in range(SUB):
                col = jnp.broadcast_to(b[:, lev.ox + x:lev.ox + x + 1], (SUB, LN))
                for j in range(4):
                    acc[j] = acc[j] + cinv[j, pl.ds(z * 64 + x, SUB, stride=SUB), :] * col
            return tuple(acc)
        acc = lax.fori_loop(0, SUB, zstep, (jnp.zeros((SUB, LN), F32),) * 4)
        lines = [jnp.broadcast_to(jnp.sum(a, axis=0, keepdims=True), (SUB, LN)) for a in acc]
        own = (lane >= lev.ox) & (lane < lev.ox + SUB)
        for z in range(SUB):
            idx = jnp.clip((z % 2) * 64 + row * SUB + lane - lev.ox, 0, 127)
            e5[lev.oz + z, pl.ds(lev.oy, SUB), :] = jnp.where(own, jnp.take_along_axis(lines[z // 2], idx, axis=1), 0.0)
        zghost(lev, e5)

    def base_of(lev):
        return (lev.oz, lev.oy, lev.ox)

    def local_visit(fine, v, rhs, descend, ecoarse, coarse, cbase):
        sweep(fine, rhs, v.at[0], None)
        zghost(fine, v.at[0])
        residual_pass(fine, v.at[0], rhs)
        descend()
        prolong_add(fine, coarse, ecoarse, v.at[0], cbase)
        loop(2, lambda i: sweep(fine, v.at[i], v.at[1 - i], rhs))

    def descend4():
        restrict_to(levels[4], levels[5], b5, None)
        coarse_solve()

    def descend3():
        restrict_to(levels[3], levels[4], b4, None)
        zghost(levels[4], b4)
        local_visit(levels[4], v4, b4, descend4, e5, levels[5], base_of(levels[5]))

    def descend2():
        restrict_packed(levels[2], me)
        gather3()
        local_visit(levels[3], v3, b3, descend3, v4.at[0], levels[4], base_of(levels[4]))

    def descend1():
        restrict_to(levels[1], levels[2], b2, p2s)
        exchange_wide(levels[2], b2, p2s, p2r, 10)
        oz, oy, ox = base_of(levels[3])
        local_visit(levels[2], v2, b2, descend2, v3.at[0], levels[3], (oz + GRP * pz, oy + GRP * py, ox + GRP * px))

    def skew_in(t):
        for copy in load(t):
            copy.wait()
        rows, frows = pl.ds(tile(t + 1), SUB), pl.ds(tile(t), SUB)
        pk = nil
        for z in range(LN):
            moved = pltpu.roll(ua[z + 1, rows, :], z, 1)
            ua[z + 1, rows, :] = moved
            pk = jnp.where(face_lane == z, moved, pk)
            fr[z, frows, :] = pltpu.roll(fr[z, frows, :] * INV_G2, z, 1)
        xs[0, frows, :] = pk
    loop(GRP, skew_in)
    for copy in load_c:
        copy.wait()

    def correct():
        exchange0(ua, 0)
        residual0()
        restrict_to(lev0, levels[1], b1, p1s)
        exchange_wide(levels[1], b1, p1s, p1r, 6)
        local_visit(levels[1], v1, b1, descend1, v2.at[0], levels[2], base_of(levels[2]))
        prolong_add(lev0, levels[1], v1.at[0], ua, base_of(levels[1]))

    def half_cycle(h):
        exchange0(ua, 0)
        sweep0(ua, ub, 0)
        exchange0(ub, 1)
        sweep0(ub, ua, 1)
        pl.when(h % 2 == 0)(correct)
    loop(2 * CYCLES, half_cycle)

    def store(t):
        return pltpu.make_async_copy(ub.at[pl.ds(1, LN), pl.ds(tile(t + 1), SUB), :], out_hbm.at[:, pl.ds(tile(t), SUB), :],
                                     lsem.at[t])

    def skew_out(t):
        rows = pl.ds(tile(t + 1), SUB)
        for z in range(LN):
            ub[z + 1, rows, :] = pltpu.roll(ua[z + 1, rows, :], -z % LN, 1)
        store(t).start()
    loop(GRP, skew_out)
    loop(GRP, lambda t: store(t).wait())


def solution(mesh):
    grid_spec = P(('batch', 'gz'), 'gy', 'gx')

    def vmem(*shape):
        return pltpu.VMEM(shape, F32)

    scratch = [vmem(130, 144, LN), vmem(130, 144, LN), vmem(LN, LN, LN), vmem(66, 144, LN), vmem(66, 80, LN), vmem(LN, SUB, LN)]
    for shape in ((82, 96), (50, 64), (34, 72), (18, 48)):
        scratch += [vmem(2, *shape, LN), vmem(*shape, LN)]
    scratch += [vmem(10, 32, LN), vmem(10, 32, LN), vmem(4, 512, LN)]
    scratch += [vmem(2, LN, LN)] * 4
    scratch += [vmem(4, 64, LN)] * 2 + [vmem(2, 32, LN)] * 2 + [vmem(SUB, 2, GRP, LN)]
    scratch += [pltpu.SemaphoreType.DMA((22,)), pltpu.SemaphoreType.DMA((22,)), pltpu.SemaphoreType.DMA((36,))]

    call = pl.pallas_call(
        solve_kernel,
        out_shape=jax.ShapeDtypeStruct((LN, LN, LN), F32),
        in_specs=[pl.BlockSpec(memory_space=pl.ANY)] * 3,
        out_specs=pl.BlockSpec(memory_space=pl.ANY),
        scratch_shapes=scratch,
        name='multigrid',
        compiler_params=pltpu.CompilerParams(collective_id=0, has_side_effects=True, vmem_limit_bytes=67043328),
    )
    return jax.shard_map(call, mesh=mesh, in_specs=(grid_spec, grid_spec, P()), out_specs=grid_spec, check_vma=False)
```

time: 745 us -> 307 us (0.41)
  Pallas kernels: 737 us -> 299 us
    pallas_call x1, Pallas kernels: 737 us -> 299 us
where the time goes in v2:
time: 307 us
  Pallas kernels  299 us (97%)
  local copies, waits for them, and re-layouts  7.89 us (3%)
    pallas_call x1, Pallas kernels  299 us
    unnamed x1, local copies, waits for them, and re-layouts  7.89 us

profile of v2, /device:TPU:0, one launch (start us, length us, event | category | flops | bytes accessed | tf_op | source)
XLA Modules:
  0.0 306.8 jit_solution(12582855683191746627)
XLA Ops:
  0.0 298.9 %multigrid.1 = f32[128,128,128]{2,1,0:T(8,128)} custom-call(f32[128,128,128]{2,1,0:T(8,128)} %f_hbm.1, f32[128,128,128]{2,1,0:T(8,128)} %u_hbm.1, f32[512,512]{1,0:T(8,128)} %c_hbm.1), custom_call_target="tpu_custom_call" | custom-call | tf_op jit(solution)/shard_map/multigrid/pallas_call
  298.9 7.9 %copy.5 = f32[128,128,128]{2,1,0:T(8,128)} copy(f32[128,128,128]{2,1,0:T(8,128)} %multigrid.1) | data formatting | bytes 16777216

commit v3 on v2

--- a/solution.py
+++ b/solution.py
@@ -39,8 +39,8 @@
 
 
 def solve_kernel(f_hbm, u_hbm, c_hbm, out_hbm,
-                 ua, ub, fr, tr, xr, sx, v1, b1, v2, b2, v3, b3, v4, b4, e5, b5, cinv,
-                 xs, xg, yp, yg, p1s, p1r, p2s, p2r, g3, ssem, rsem, lsem):
+                 ua, ub, fr, tr, xr, sx, sy, v1, b1, v2, b2, v3, b3, v4, b4, e5, b5, cinv,
+                 xs, xg, yp, yg, p1s, p1r, p2s, p2r, g3, ssem, rsem, xss, xrs, zss, zrs, lsem):
     pz, py, px = lax.axis_index('gz'), lax.axis_index('gy'), lax.axis_index('gx')
     pos = (pz, py, px)
     lane = lax.broadcasted_iota(jnp.int32, (SUB, LN), 1)
@@ -87,7 +87,7 @@
     def start_load(t):
         for copy in load(t):
             copy.start()
-    loop(GRP, start_load)
+    loop(GRP, lambda t: start_load(jnp.where(py == 0, 15 - t, t)))
     load_c = [pltpu.make_async_copy(c_hbm.at[:, pl.ds(LN * j, LN)], cinv.at[j], lsem.at[32 + j]) for j in range(4)]
     for copy in load_c:
         copy.start()
@@ -187,7 +187,50 @@
             blocks(lev.n // SUB, max(1, lev.n // GRP // 2), block)
         loop(lev.n // SUB, ytile)
 
-    def roll_sums0(src, par, t):
+    zface = jnp.where(pz == 0, LN, 1)
+    zdst = LN + 1 - zface + jnp.where(pz == 0, -1, 1)
+    yface = jnp.where(py == 0, 135, SUB)
+    yghost = jnp.where(py == 0, 136, 7)
+
+    def order(t):
+        return jnp.where(py == 0, 15 - t, t)
+
+    def pieces(buf, par, o):
+        rows, yrows = pl.ds(tile(o), SUB), pl.ds(tile(o + 1), SUB)
+        return (pltpu.make_async_remote_copy(src_ref=xs.at[par, rows, :], dst_ref=xg.at[par, rows, :], send_sem=xss.at[par, o],
+                                             recv_sem=xrs.at[par, o], device_id=dev(1), device_id_type=MESH),
+                pltpu.make_async_remote_copy(src_ref=buf.at[zface, yrows, :], dst_ref=buf.at[zdst, yrows, :],
+                                             send_sem=zss.at[par, o], recv_sem=zrs.at[par, o], device_id=dev(4),
+                                             device_id_type=MESH))
+
+    def face_rows(par):
+        return remote(yp.at[par], yg.at[par], par, 2)
+
+    def send(buf, par, t):
+        for copy in pieces(buf, par, order(t)):
+            copy.start()
+
+        def first():
+            def take_rows(i):
+                for j in range(SUB):
+                    yp[par, pl.ds(SUB * i + j, 1), :] = buf[SUB * i + j + 1, pl.ds(yface, 1), :]
+            loop(GRP, take_rows)
+            face_rows(par).start()
+        pl.when(t == 0)(first)
+
+    def receive(buf, par, t):
+        def first():
+            face_rows(par).wait()
+
+            def put_rows(i):
+                for j in range(SUB):
+                    buf[SUB * i + j + 1, pl.ds(yghost, 1), :] = yg[par, pl.ds(SUB * i + j, 1), :]
+            loop(GRP, put_rows)
+        pl.when(t == 0)(first)
+        for copy in pieces(buf, par, order(t)):
+            copy.wait()
+
+    def roll_sums0(src, par, t, sx):
         rows = pl.ds(tile(t + 1), SUB)
         ghost = xg[par, pl.ds(tile(t), SUB), :]
         left = jnp.where(low_x, 0.0, ghost)
@@ -206,7 +249,7 @@
             sx[z] = s
             below, here = here, above
 
-    def cells0(src, t, z):
+    def cells0(src, t, z, sx):
         y0, planes = tile(t + 1), pl.ds(z + 1, GRP)
         s = sx[pl.ds(z, GRP)] + src[planes, pl.ds(y0 - 1, SUB), :] + src[planes, pl.ds(y0 + 1, SUB), :]
         return src[planes, pl.ds(y0, SUB), :], s + fr[pl.ds(z, GRP), pl.ds(tile(t), SUB), :]
@@ -217,27 +260,32 @@
 
     def sweep0(src, dst, par):
         def ytile(t):
-            roll_sums0(src, par, t)
-            cc = (1.0 - OMEGA) - C6 * yedge(t)
+            receive(src, par, t)
+            o = order(t)
+            roll_sums0(src, par, o, sx)
+            cc = (1.0 - OMEGA) - C6 * yedge(o)
 
             def block(k, pk):
-                c, s = cells0(src, t, GRP * k)
+                c, s = cells0(src, o, GRP * k, sx)
                 new = cc * c + C6 * s
-                dst[pl.ds(GRP * k + 1, GRP), pl.ds(tile(t + 1), SUB), :] = new
+                dst[pl.ds(GRP * k + 1, GRP), pl.ds(tile(o + 1), SUB), :] = new
                 for j in range(GRP):
                     pk = jnp.where(face_lane == GRP * k + j, new[j], pk)
                 return pk
-            xs[1 - par, pl.ds(tile(t), SUB), :] = lax.fori_loop(0, SUB, block, nil)
+            xs[1 - par, pl.ds(tile(o), SUB), :] = lax.fori_loop(0, SUB, block, nil)
+            send(dst, 1 - par, t)
         loop(GRP, ytile)
 
     def residual0():
         def ytile(t):
-            roll_sums0(ua, 0, t)
-            dd = 6.0 + yedge(t)
+            receive(ua, 0, t)
+            o = order(t)
+            roll_sums0(ua, 0, o, sx)
+            dd = 6.0 + yedge(o)
 
             def block(k):
-                c, s = cells0(ua, t, GRP * k)
-                ub[pl.ds(GRP * k + 1, GRP), pl.ds(tile(t + 1), SUB), :] = s - dd * c
+                c, s = cells0(ua, o, GRP * k, sx)
+                ub[pl.ds(GRP * k + 1, GRP), pl.ds(tile(o + 1), SUB), :] = s - dd * c
             loop(SUB, block)
         loop(GRP, ytile)
 
@@ -321,10 +369,12 @@
                 xr[z, pl.ds(SUB * t, SUB), :] = (wx * jnp.take_along_axis(v, i0, axis=1)
                                                  + wn * jnp.take_along_axis(v, i1, axis=1))
 
-        def spread_two(z):
-            spread(2 * z)
-            spread(2 * z + 1)
-        loop(ncz // 2, spread_two)
+        per = 6 if ncz % 6 == 0 else 2
+
+        def spread_some(i):
+            for q in range(per):
+                spread(per * i + q)
+        loop(ncz // per, spread_some)
 
         def ctile(t):
             fy = pl.multiple_of(fy_s + GRP * t, SUB)
@@ -335,16 +385,17 @@
             wdo = jnp.where(iny, jnp.where(r == coarse.hi[1] - 1, 0.5, 0.75), 0.0)
 
             def plane(i):
-                for q in range(2):
-                    z = 2 * i + q
+                for q in range(per):
+                    z = per * i + q
                     e = xr[z, pl.ds(tile(t + 1), SUB), :]
                     tr[z, pl.ds(fy, SUB, stride=2), :] = wde * e + wny * xr[z, pl.ds(tile(t + 1) - 1, SUB), :]
                     tr[z, pl.ds(fy + 1, SUB, stride=2), :] = wdo * e + wny * xr[z, pl.ds(tile(t + 1) + 1, SUB), :]
-            loop(ncz // 2, plane)
+            loop(ncz // per, plane)
         loop(nct, ctile)
 
         def ytile(t):
-            y0 = pl.multiple_of(fine.ys + SUB * t, SUB)
+            o = t if fine.idx else order(t)
+            y0 = pl.multiple_of(fine.ys + SUB * o, SUB)
             rows = pl.ds(y0, SUB)
             pk = nil
             for k in range(fine.nzb):
@@ -363,34 +414,9 @@
             if fine.idx:
                 zghost_tile(fine, dst, y0)
             else:
-                xs[0, pl.ds(tile(t), SUB), :] = pk
+                xs[0, pl.ds(tile(o), SUB), :] = pk
+                send(dst, 0, t)
         loop(fine.nyt, ytile)
-
-    zface = jnp.where(pz == 0, LN, 1)
-    zdst = LN + 1 - zface + jnp.where(pz == 0, -1, 1)
-    yface = jnp.where(py == 0, 135, SUB)
-    yghost = jnp.where(py == 0, 136, 7)
-
-    def exchange0(buf, par):
-        cx = remote(xs.at[par], xg.at[par], par, 1)
-        cx.start()
-        cz = remote(buf.at[zface, pl.ds(SUB, LN), :], buf.at[zdst, pl.ds(SUB, LN), :], 2 + par, 4)
-        cz.start()
-
-        def take_rows(i):
-            for j in range(SUB):
-                yp[par, pl.ds(SUB * i + j, 1), :] = buf[SUB * i + j + 1, pl.ds(yface, 1), :]
-        loop(GRP, take_rows)
-        cy = remote(yp.at[par], yg.at[par], 4 + par, 2)
-        cy.start()
-        cy.wait()
-
-        def put_rows(i):
-            for j in range(SUB):
-                buf[SUB * i + j + 1, pl.ds(yghost, 1), :] = yg[par, pl.ds(SUB * i + j, 1), :]
-        loop(GRP, put_rows)
-        cx.wait()
-        cz.wait()
 
     def exchange_wide(lev, ref, sendp, recvp, k):
         n, h = lev.n, HALO_PLANES[lev.idx]
@@ -501,9 +527,10 @@
         local_visit(levels[2], v2, b2, descend2, v3.at[0], levels[3], (oz + GRP * pz, oy + GRP * py, ox + GRP * px))
 
     def skew_in(t):
-        for copy in load(t):
+        o = order(t)
+        for copy in load(o):
             copy.wait()
-        rows, frows = pl.ds(tile(t + 1), SUB), pl.ds(tile(t), SUB)
+        rows, frows = pl.ds(tile(o + 1), SUB), pl.ds(tile(o), SUB)
         pk = nil
         for z in range(LN):
             moved = pltpu.roll(ua[z + 1, rows, :], z, 1)
@@ -511,12 +538,12 @@
             pk = jnp.where(face_lane == z, moved, pk)
             fr[z, frows, :] = pltpu.roll(fr[z, frows, :] * INV_G2, z, 1)
         xs[0, frows, :] = pk
+        send(ua, 0, t)
     loop(GRP, skew_in)
     for copy in load_c:
         copy.wait()
 
     def correct():
-        exchange0(ua, 0)
         residual0()
         restrict_to(lev0, levels[1], b1, p1s)
         exchange_wide(levels[1], b1, p1s, p1r, 6)
@@ -524,12 +551,11 @@
         prolong_add(lev0, levels[1], v1.at[0], ua, base_of(levels[1]))
 
     def half_cycle(h):
-        exchange0(ua, 0)
         sweep0(ua, ub, 0)
-        exchange0(ub, 1)
         sweep0(ub, ua, 1)
         pl.when(h % 2 == 0)(correct)
     loop(2 * CYCLES, half_cycle)
+    loop(GRP, lambda t: receive(ua, 0, t))
 
     def store(t):
         return pltpu.make_async_copy(ub.at[pl.ds(1, LN), pl.ds(tile(t + 1), SUB), :], out_hbm.at[:, pl.ds(tile(t), SUB), :],
@@ -550,13 +576,14 @@
     def vmem(*shape):
         return pltpu.VMEM(shape, F32)
 
-    scratch = [vmem(130, 144, LN), vmem(130, 144, LN), vmem(LN, LN, LN), vmem(66, 144, LN), vmem(66, 80, LN), vmem(LN, SUB, LN)]
+    scratch = [vmem(130, 144, LN), vmem(130, 144, LN), vmem(LN, LN, LN), vmem(66, 144, LN), vmem(66, 80, LN), vmem(LN, SUB, LN), vmem(LN, SUB, LN)]
     for shape in ((82, 96), (50, 64), (34, 72), (18, 48)):
         scratch += [vmem(2, *shape, LN), vmem(*shape, LN)]
     scratch += [vmem(10, 32, LN), vmem(10, 32, LN), vmem(4, 512, LN)]
     scratch += [vmem(2, LN, LN)] * 4
     scratch += [vmem(4, 64, LN)] * 2 + [vmem(2, 32, LN)] * 2 + [vmem(SUB, 2, GRP, LN)]
-    scratch += [pltpu.SemaphoreType.DMA((22,)), pltpu.SemaphoreType.DMA((22,)), pltpu.SemaphoreType.DMA((36,))]
+    scratch += [pltpu.SemaphoreType.DMA((22,)), pltpu.SemaphoreType.DMA((22,))]
+    scratch += [pltpu.SemaphoreType.DMA((2, GRP))] * 4 + [pltpu.SemaphoreType.DMA((36,))]
 
     call = pl.pallas_call(
         solve_kernel,

time: 307 us -> 273 us (0.89)
  Pallas kernels: 299 us -> 265 us
    pallas_call x1, Pallas kernels: 299 us -> 265 us
where the time goes in v3:
time: 273 us
  Pallas kernels  265 us (97%)
  local copies, waits for them, and re-layouts  7.89 us (3%)
    pallas_call x1, Pallas kernels  265 us
    unnamed x1, local copies, waits for them, and re-layouts  7.89 us

profile of v3, /device:TPU:0, one launch (start us, length us, event | category | flops | bytes accessed | tf_op | source)
XLA Modules:
  0.0 272.5 jit_solution(18189445759612817979)
XLA Ops:
  0.0 264.6 %multigrid.1 = f32[128,128,128]{2,1,0:T(8,128)} custom-call(f32[128,128,128]{2,1,0:T(8,128)} %f_hbm.1, f32[128,128,128]{2,1,0:T(8,128)} %u_hbm.1, f32[512,512]{1,0:T(8,128)} %c_hbm.1), custom_call_target="tpu_custom_call" | custom-call | tf_op jit(solution)/shard_map/multigrid/pallas_call
  264.6 7.9 %copy.5 = f32[128,128,128]{2,1,0:T(8,128)} copy(f32[128,128,128]{2,1,0:T(8,128)} %multigrid.1) | data formatting | bytes 16777216

commit v4 on v3

--- a/solution.py
+++ b/solution.py
@@ -59,6 +59,9 @@
     face_lane = jnp.where(low_x, (lane + 1) & BACK, lane)
     out_lane = jnp.where(low_x, lane, (lane + 1) & BACK)
 
+    skew = (lax.broadcasted_iota(jnp.int32, (SUB, SUB, LN), 2) - lax.broadcasted_iota(jnp.int32, (SUB, SUB, LN), 0)) & BACK
+    out_skew = jnp.where(low_x, skew, (skew + 1) & BACK)
+
     def dev(code):
         ids = {}
         if code & 4:
@@ -236,18 +239,16 @@
         left = jnp.where(low_x, 0.0, ghost)
         right = jnp.where(low_x, ghost, 0.0)
         zlow = jnp.where(pz == 0, 1.0, 0.0)
-        below, here = src[0, rows, :], src[1, rows, :]
-        for z in range(LN):
-            above = src[z + 2, rows, :]
-            a = jnp.where(lane == (z - 1) % LN, left, here) + below
-            b = jnp.where(lane == z, right, here) + above
-            s = pltpu.roll(a, 1, 1) + pltpu.roll(b, BACK, 1) - jnp.where(out_lane == z, here, 0.0)
-            if z == 0:
-                s = s - zlow * here
-            if z == LN - 1:
-                s = s - (1.0 - zlow) * here
-            sx[z] = s
-            below, here = here, above
+        for k in range(GRP):
+            z = SUB * k
+            v = src[pl.ds(z, SUB + 2), rows, :]
+            here = v[1:SUB + 1]
+            a = jnp.where(skew == (z - 1) % LN, left[None], here) + v[0:SUB]
+            b = jnp.where(skew == z, right[None], here) + v[2:SUB + 2]
+            s = pltpu.roll(a, 1, 2) + pltpu.roll(b, BACK, 2) - jnp.where(out_skew == z, here, 0.0)
+            sx[pl.ds(z, SUB)] = s
+        sx[0] = sx[0] - zlow * src[1, rows, :]
+        sx[BACK] = sx[BACK] - (1.0 - zlow) * src[LN, rows, :]
 
     def cells0(src, t, z, sx):
         y0, planes = tile(t + 1), pl.ds(z + 1, GRP)
@@ -258,36 +259,45 @@
         r = row + tile(t + 1)
         return jnp.where((r == lev0.lo[1]) | (r == lev0.hi[1] - 1), 1.0, 0.0)
 
+    def tiles0(src, par, work):
+        receive(src, par, 0)
+        roll_sums0(src, par, order(0), sx)
+
+        def step(t):
+            pl.when(t < 15)(lambda: receive(src, par, t + 1))
+
+            def both(now, later):
+                roll_sums0(src, par, order(t + 1 - (t + 1) // GRP), later)
+                work(order(t), now)
+            pl.when(t % 2 == 0)(lambda: both(sx, sy))
+            pl.when(t % 2 == 1)(lambda: both(sy, sx))
+            work_done(t)
+
+        work_done = work.done
+        loop(GRP, step)
+
     def sweep0(src, dst, par):
-        def ytile(t):
-            receive(src, par, t)
-            o = order(t)
-            roll_sums0(src, par, o, sx)
+        def work(o, sums):
             cc = (1.0 - OMEGA) - C6 * yedge(o)
-
-            def block(k, pk):
-                c, s = cells0(src, o, GRP * k, sx)
+            pk = nil
+            for k in range(SUB):
+                c, s = cells0(src, o, GRP * k, sums)
                 new = cc * c + C6 * s
                 dst[pl.ds(GRP * k + 1, GRP), pl.ds(tile(o + 1), SUB), :] = new
                 for j in range(GRP):
                     pk = jnp.where(face_lane == GRP * k + j, new[j], pk)
-                return pk
-            xs[1 - par, pl.ds(tile(o), SUB), :] = lax.fori_loop(0, SUB, block, nil)
-            send(dst, 1 - par, t)
-        loop(GRP, ytile)
+            xs[1 - par, pl.ds(tile(o), SUB), :] = pk
+        work.done = lambda t: send(dst, 1 - par, t)
+        tiles0(src, par, work)
 
     def residual0():
-        def ytile(t):
-            receive(ua, 0, t)
-            o = order(t)
-            roll_sums0(ua, 0, o, sx)
+        def work(o, sums):
             dd = 6.0 + yedge(o)
-
-            def block(k):
-                c, s = cells0(ua, o, GRP * k, sx)
+            for k in range(SUB):
+                c, s = cells0(ua, o, GRP * k, sums)
                 ub[pl.ds(GRP * k + 1, GRP), pl.ds(tile(o + 1), SUB), :] = s - dd * c
-            loop(SUB, block)
-        loop(GRP, ytile)
+        work.done = lambda t: None
+        tiles0(ua, 0, work)
 
     def pair_sums(fine, j):
         for zc in range(fine.n // 2):
@@ -308,25 +318,23 @@
         idx = (fine.ox + 2 * (lane - coarse.ox)) & BACK
         pidx = fine.ox + 2 * (jnp.where(low_x, half - SUB, 0) + lane % SUB)
         group = lane // SUB
-        step = min(GRP, half // 2)
+        step = half // 2
 
         def ytile(j):
             rows = pl.ds(pl.multiple_of(coarse.oy + SUB * j, SUB), SUB)
             pair_sums(fine, j)
 
             def move(q):
+                pk = nil
                 for i in range(step):
                     z = step * q + i
-                    dst[coarse.oz + z, rows, :] = jnp.where(own, jnp.take_along_axis(sx[z], idx, axis=1), 0.0)
-            loop(half // step, move)
-
-            def collect(q):
-                pk = nil
-                for i in range(GRP):
-                    pk = jnp.where(group == i, jnp.take_along_axis(sx[GRP * q + i], pidx, axis=1), pk)
-                pack[q, pl.ds(tile(j), SUB), :] = pk
-            if pack is not None:
-                loop(half // GRP, collect)
+                    v = sx[z]
+                    dst[coarse.oz + z, rows, :] = jnp.where(own, jnp.take_along_axis(v, idx, axis=1), 0.0)
+                    if pack is not None:
+                        pk = jnp.where(group == i % GRP, jnp.take_along_axis(v, pidx, axis=1), pk)
+                        if i % GRP == GRP - 1:
+                            pack[q * (step // GRP) + i // GRP, pl.ds(tile(j), SUB), :] = pk
+            loop(2, move)
         loop(half // SUB, ytile)
 
     def restrict_packed(fine, me):

time: 273 us -> 252 us (0.923)
  Pallas kernels: 265 us -> 244 us
    pallas_call x1, Pallas kernels: 265 us -> 244 us
where the time goes in v4:
time: 252 us
  Pallas kernels  244 us (97%)
  local copies, waits for them, and re-layouts  7.89 us (3%)
    pallas_call x1, Pallas kernels  244 us
    unnamed x1, local copies, waits for them, and re-layouts  7.89 us

profile of v4, /device:TPU:0, one launch (start us, length us, event | category | flops | bytes accessed | tf_op | source)
XLA Modules:
  0.0 251.7 jit_solution(7154973594279745628)
XLA Ops:
  0.0 243.8 %multigrid.1 = f32[128,128,128]{2,1,0:T(8,128)} custom-call(f32[128,128,128]{2,1,0:T(8,128)} %f_hbm.1, f32[128,128,128]{2,1,0:T(8,128)} %u_hbm.1, f32[512,512]{1,0:T(8,128)} %c_hbm.1), custom_call_target="tpu_custom_call" | custom-call | tf_op jit(solution)/shard_map/multigrid/pallas_call
  243.8 7.9 %copy.5 = f32[128,128,128]{2,1,0:T(8,128)} copy(f32[128,128,128]{2,1,0:T(8,128)} %multigrid.1) | data formatting | bytes 16777216

commit v5 on v4

--- a/solution.py
+++ b/solution.py
@@ -10,7 +10,7 @@
 CYCLES = 2
 MESH = pl.DeviceIdType.MESH
 F32 = jnp.float32
-SUB, GRP, LN = 8, 16, 128
+PAIR, SUB, GRP, LN = 2, 8, 16, 128
 HALO_PLANES = {1: 4, 2: 5}
 BACK = LN - 1
 INV_G2 = 1.0 / 65536.0
@@ -23,7 +23,7 @@
         self.split = split
         if split:
             self.lo = tuple(o - p * n for o, p in zip(off, pos))
-            self.hi = tuple(l + 2 * n for l in self.lo)
+            self.hi = tuple(l + PAIR * n for l in self.lo)
         else:
             self.lo = off
             self.hi = tuple(o + n for o in off)
@@ -40,7 +40,7 @@
 
 def solve_kernel(f_hbm, u_hbm, c_hbm, out_hbm,
                  ua, ub, fr, tr, xr, sx, sy, v1, b1, v2, b2, v3, b3, v4, b4, e5, b5, cinv,
-                 xs, xg, yp, yg, p1s, p1r, p2s, p2r, g3, ssem, rsem, xss, xrs, zss, zrs, lsem):
+                 xs, xg, yp, yg, p1s, p1r, p2s, p2r, h1s, h1r, h2s, h2r, g3, ssem, rsem, xss, xrs, zss, zrs, wss, wrs, lsem):
     pz, py, px = lax.axis_index('gz'), lax.axis_index('gy'), lax.axis_index('gx')
     pos = (pz, py, px)
     lane = lax.broadcasted_iota(jnp.int32, (SUB, LN), 1)
@@ -49,7 +49,7 @@
     levels = [
         Level(0, LN, (1, SUB, 0), (130, 144), pos, True),
         Level(1, 64, (9, GRP, 32), (82, 96), pos, True),
-        Level(2, 32, (9, GRP, 48), (50, 64), pos, True),
+        Level(PAIR, 32, (9, GRP, 48), (50, 64), pos, True),
         Level(3, 32, (1, GRP, 48), (34, 72), pos, False),
         Level(4, GRP, (1, GRP, 48), (18, 48), pos, False),
         Level(5, SUB, (1, GRP, 48), (10, 32), pos, False),
@@ -59,14 +59,14 @@
     face_lane = jnp.where(low_x, (lane + 1) & BACK, lane)
     out_lane = jnp.where(low_x, lane, (lane + 1) & BACK)
 
-    skew = (lax.broadcasted_iota(jnp.int32, (SUB, SUB, LN), 2) - lax.broadcasted_iota(jnp.int32, (SUB, SUB, LN), 0)) & BACK
+    skew = (lax.broadcasted_iota(jnp.int32, (SUB, SUB, LN), PAIR) - lax.broadcasted_iota(jnp.int32, (SUB, SUB, LN), 0)) & BACK
     out_skew = jnp.where(low_x, skew, (skew + 1) & BACK)
 
     def dev(code):
         ids = {}
         if code & 4:
             ids['gz'] = 1 - pz
-        if code & 2:
+        if code & PAIR:
             ids['gy'] = 1 - py
         if code & 1:
             ids['gx'] = 1 - px
@@ -122,10 +122,10 @@
 
     def coefs(lev, y0):
         r = row + y0
-        inside = (r >= lev.lo[1]) & (r < lev.hi[1]) & (lane >= lev.lo[2]) & (lane < lev.hi[2])
+        inside = (r >= lev.lo[1]) & (r < lev.hi[1]) & (lane >= lev.lo[PAIR]) & (lane < lev.hi[PAIR])
         one = jnp.ones((SUB, LN), F32)
         nb = (jnp.where(r == lev.lo[1], one, nil) + jnp.where(r == lev.hi[1] - 1, one, nil)
-              + jnp.where(lane == lev.lo[2], one, nil) + jnp.where(lane == lev.hi[2] - 1, one, nil))
+              + jnp.where(lane == lev.lo[PAIR], one, nil) + jnp.where(lane == lev.hi[PAIR] - 1, one, nil))
         return inside, nb
 
     def zghost_tile(lev, ref, y0):
@@ -135,21 +135,21 @@
     def zghost(lev, ref):
         loop(lev.shape[1] // SUB, lambda t: zghost_tile(lev, ref, tile(t)))
 
-    def blocks(count, per, body):
+    def several(count, per, body):
         def step(i):
             for k in range(per):
                 body(i * per + k)
         loop(count // per, step)
 
     def roll_sums(src, zs, nzb, y0):
-        for z in range(SUB * nzb):
-            c = src[zs + z, pl.ds(y0, SUB), :]
-            sx[z] = pltpu.roll(c, 1, 1) + pltpu.roll(c, BACK, 1)
+        for k in range(nzb):
+            c = src[pl.ds(zs + SUB * k, SUB), pl.ds(y0, SUB), :]
+            sx[pl.ds(SUB * k, SUB)] = pltpu.roll(c, 1, PAIR) + pltpu.roll(c, BACK, PAIR)
 
     def stencil(src, zs, k, y0):
         z0 = zs + SUB * k
-        v = src[pl.ds(z0 - 1, SUB + 2), pl.ds(y0, SUB), :]
-        s = v[0:SUB] + v[2:SUB + 2]
+        v = src[pl.ds(z0 - 1, SUB + PAIR), pl.ds(y0, SUB), :]
+        s = v[0:SUB] + v[PAIR:SUB + PAIR]
         s = s + src[pl.ds(z0, SUB), pl.ds(y0 - 1, SUB), :] + src[pl.ds(z0, SUB), pl.ds(y0 + 1, SUB), :]
         return v[1:SUB + 1], s + sx[pl.ds(SUB * k, SUB)]
 
@@ -172,7 +172,7 @@
                 if not first:
                     s = s + rhs[pl.ds(z0, SUB), pl.ds(y0, SUB), :]
                 dst[pl.ds(z0, SUB), pl.ds(y0, SUB), :] = ca * c + cb * s
-            blocks(lev.nzb, 3 if lev.nzb == 9 else 2 if lev.nzb == 4 else 1, block)
+            several(lev.nzb, 3 if lev.nzb == 9 else PAIR if lev.nzb == 4 else 1, block)
             zghost_tile(lev, dst, y0)
         loop(lev.nyt, ytile)
 
@@ -185,9 +185,9 @@
 
             def block(k):
                 c, s = stencil(src, lev.oz, k, y0)
-                r = (rhs[pl.ds(lev.oz + SUB * k, SUB), pl.ds(y0, SUB), :] + (s - dd * c)).reshape(4, 2, SUB, LN)
+                r = (rhs[pl.ds(lev.oz + SUB * k, SUB), pl.ds(y0, SUB), :] + (s - dd * c)).reshape(4, PAIR, SUB, LN)
                 tr[pl.ds(4 * k, 4), pl.ds(tile(t), SUB), :] = r[:, 0] + r[:, 1]
-            blocks(lev.n // SUB, max(1, lev.n // GRP // 2), block)
+            several(lev.n // SUB, max(1, lev.n // GRP // PAIR), block)
         loop(lev.n // SUB, ytile)
 
     zface = jnp.where(pz == 0, LN, 1)
@@ -207,7 +207,7 @@
                                              device_id_type=MESH))
 
     def face_rows(par):
-        return remote(yp.at[par], yg.at[par], par, 2)
+        return remote(yp.at[par], yg.at[par], par, PAIR)
 
     def send(buf, par, t):
         for copy in pieces(buf, par, order(t)):
@@ -241,11 +241,11 @@
         zlow = jnp.where(pz == 0, 1.0, 0.0)
         for k in range(GRP):
             z = SUB * k
-            v = src[pl.ds(z, SUB + 2), rows, :]
+            v = src[pl.ds(z, SUB + PAIR), rows, :]
             here = v[1:SUB + 1]
             a = jnp.where(skew == (z - 1) % LN, left[None], here) + v[0:SUB]
-            b = jnp.where(skew == z, right[None], here) + v[2:SUB + 2]
-            s = pltpu.roll(a, 1, 2) + pltpu.roll(b, BACK, 2) - jnp.where(out_skew == z, here, 0.0)
+            b = jnp.where(skew == z, right[None], here) + v[PAIR:SUB + PAIR]
+            s = pltpu.roll(a, 1, PAIR) + pltpu.roll(b, BACK, PAIR) - jnp.where(out_skew == z, here, 0.0)
             sx[pl.ds(z, SUB)] = s
         sx[0] = sx[0] - zlow * src[1, rows, :]
         sx[BACK] = sx[BACK] - (1.0 - zlow) * src[LN, rows, :]
@@ -269,8 +269,8 @@
             def both(now, later):
                 roll_sums0(src, par, order(t + 1 - (t + 1) // GRP), later)
                 work(order(t), now)
-            pl.when(t % 2 == 0)(lambda: both(sx, sy))
-            pl.when(t % 2 == 1)(lambda: both(sy, sx))
+            pl.when(t % PAIR == 0)(lambda: both(sx, sy))
+            pl.when(t % PAIR == 1)(lambda: both(sy, sx))
             work_done(t)
 
         work_done = work.done
@@ -300,27 +300,28 @@
         tiles0(ua, 0, work)
 
     def pair_sums(fine, j):
-        for zc in range(fine.n // 2):
-            lo, hi = pl.ds(GRP * j, SUB, stride=2), pl.ds(GRP * j + 1, SUB, stride=2)
+        for zc in range(fine.n // PAIR):
+            lo, hi = pl.ds(GRP * j, SUB, stride=PAIR), pl.ds(GRP * j + 1, SUB, stride=PAIR)
             if fine.idx:
                 s = tr[zc, lo, :] + tr[zc, hi, :]
                 sx[zc] = 0.5 * (s + pltpu.roll(s, BACK, 1))
                 continue
-            lo, hi = pl.ds(GRP * j + SUB, SUB, stride=2), pl.ds(GRP * j + SUB + 1, SUB, stride=2)
-            e = ub[2 * zc + 1, lo, :] + ub[2 * zc + 1, hi, :]
-            o = ub[2 * zc + 2, lo, :] + ub[2 * zc + 2, hi, :]
-            s = pltpu.roll(e, -2 * zc % LN, 1) + pltpu.roll(e + o, (-2 * zc - 1) % LN, 1)
-            sx[zc] = 0.5 * (s + pltpu.roll(o, (-2 * zc - 2) % LN, 1))
-
-    def restrict_to(fine, coarse, dst, pack):
-        half = fine.n // 2
+            lo, hi = pl.ds(GRP * j + SUB, SUB, stride=PAIR), pl.ds(GRP * j + SUB + 1, SUB, stride=PAIR)
+            e = ub[PAIR * zc + 1, lo, :] + ub[PAIR * zc + 1, hi, :]
+            o = ub[PAIR * zc + PAIR, lo, :] + ub[PAIR * zc + PAIR, hi, :]
+            s = pltpu.roll(e, -PAIR * zc % LN, 1) + pltpu.roll(e + o, (-PAIR * zc - 1) % LN, 1)
+            sx[zc] = 0.5 * (s + pltpu.roll(o, (-PAIR * zc - PAIR) % LN, 1))
+
+    def restrict_to(fine, coarse, dst, pack=None):
+        half = fine.n // PAIR
         own = (lane >= coarse.ox) & (lane < coarse.ox + half)
-        idx = (fine.ox + 2 * (lane - coarse.ox)) & BACK
-        pidx = fine.ox + 2 * (jnp.where(low_x, half - SUB, 0) + lane % SUB)
+        idx = (fine.ox + PAIR * (lane - coarse.ox)) & BACK
+        pidx = fine.ox + PAIR * (jnp.where(low_x, half - SUB, 0) + lane % SUB)
         group = lane // SUB
-        step = half // 2
-
-        def ytile(j):
+        step = half // PAIR
+
+        def ytile(t):
+            j = t if pack is None else jnp.where(py == 0, half // SUB - 1 - t, t)
             rows = pl.ds(pl.multiple_of(coarse.oy + SUB * j, SUB), SUB)
             pair_sums(fine, j)
 
@@ -334,11 +335,36 @@
                         pk = jnp.where(group == i % GRP, jnp.take_along_axis(v, pidx, axis=1), pk)
                         if i % GRP == GRP - 1:
                             pack[q * (step // GRP) + i // GRP, pl.ds(tile(j), SUB), :] = pk
-            loop(2, move)
+            loop(PAIR, move)
+            if pack is not None:
+                copies = edge_pieces(coarse, dst, j)
+                copies[0].start()
+
+                def start_rest():
+                    for copy in copies[1:]:
+                        copy.start()
+                pl.when(t == 0)(start_rest)
         loop(half // SUB, ytile)
 
+    def wide_spans(lev):
+        n, h = lev.n, HALO_PLANES[lev.idx]
+        fy = pl.multiple_of(jnp.where(py == 0, lev.oy + n - SUB, lev.oy), SUB)
+        hy = pl.multiple_of(jnp.where(py == 0, lev.oy - SUB, lev.oy + n), SUB)
+        fz = jnp.where(pz == 0, lev.oz + n - h, lev.oz)
+        hz = jnp.where(pz == 0, lev.oz - h, lev.oz + n)
+        return fy, hy, pl.ds(fz, h), pl.ds(hz, h)
+
+    def edge_pieces(lev, ref, j):
+        fy, hy, fz, hz = wide_spans(lev)
+        rows, own, k = pl.ds(pl.multiple_of(lev.oy + SUB * j, SUB), SUB), pl.ds(lev.oz, lev.n), lev.idx
+        piece = pltpu.make_async_remote_copy(src_ref=ref.at[fz, rows, :], dst_ref=ref.at[hz, rows, :],
+                                             send_sem=wss.at[k - 1, j], recv_sem=wrs.at[k - 1, j], device_id=dev(4),
+                                             device_id_type=MESH)
+        return (piece, remote(ref.at[own, pl.ds(fy, SUB), :], ref.at[own, pl.ds(hy, SUB), :], 4 * k + 3, PAIR),
+                remote(ref.at[fz, pl.ds(fy, SUB), :], ref.at[hz, pl.ds(hy, SUB), :], 4 * k + 4, 6))
+
     def restrict_packed(fine, me):
-        idx = fine.ox + 2 * (lane % GRP)
+        idx = fine.ox + PAIR * (lane % GRP)
         group = lane // GRP
 
         def ytile(j):
@@ -349,35 +375,35 @@
                 for i in range(SUB):
                     pk = jnp.where(group == i, jnp.take_along_axis(sx[SUB * q + i], idx, axis=1), pk)
                 g3[me, q, pl.ds(tile(j), SUB), :] = pk
-            loop(2, collect)
-        loop(2, ytile)
+            loop(PAIR, collect)
+        loop(PAIR, ytile)
 
     def prolong_add(fine, coarse, esrc, dst, cbase):
-        back_z = (fine.oz - fine.zs) // 2
-        back_y = (fine.oy - fine.ys) // 2
+        back_z = (fine.oz - fine.zs) // PAIR
+        back_y = (fine.oy - fine.ys) // PAIR
         nct = fine.n // GRP + (0 if fine.nyt * SUB == fine.n else 1)
-        cy_s = cbase[1] - 2 * back_y
+        cy_s = cbase[1] - PAIR * back_y
         fy_s = fine.oy - 4 * back_y
         cz_s = cbase[0] - back_z - 1
-        ncz = 4 * fine.nzb + 2
+        ncz = 4 * fine.nzb + PAIR
         xf = lane - fine.ox
         half = lax.shift_right_arithmetic(xf, 1)
-        odd = xf - 2 * half
-        i0 = half + cbase[2]
-        i1 = jnp.clip(i0 + 2 * odd - 1, 0, BACK)
+        odd = xf - PAIR * half
+        i0 = half + cbase[PAIR]
+        i1 = jnp.clip(i0 + PAIR * odd - 1, 0, BACK)
         i0 = jnp.clip(i0, 0, BACK)
-        inx = (lane >= fine.lo[2]) & (lane < fine.hi[2])
-        edge = (lane == fine.lo[2]) | (lane == fine.hi[2] - 1)
+        inx = (lane >= fine.lo[PAIR]) & (lane < fine.hi[PAIR])
+        edge = (lane == fine.lo[PAIR]) | (lane == fine.hi[PAIR] - 1)
         wx = jnp.where(inx, jnp.where(edge, 0.5, 0.75), 0.0)
         wn = jnp.where(inx, 0.25, 0.0)
 
         def spread(z):
-            for t in range(nct + 2):
+            for t in range(nct + PAIR):
                 v = esrc[cz_s + z, pl.ds(pl.multiple_of(cy_s + SUB * (t - 1), SUB), SUB), :]
                 xr[z, pl.ds(SUB * t, SUB), :] = (wx * jnp.take_along_axis(v, i0, axis=1)
                                                  + wn * jnp.take_along_axis(v, i1, axis=1))
 
-        per = 6 if ncz % 6 == 0 else 2
+        per = 6 if ncz % 6 == 0 else PAIR
 
         def spread_some(i):
             for q in range(per):
@@ -396,8 +422,8 @@
                 for q in range(per):
                     z = per * i + q
                     e = xr[z, pl.ds(tile(t + 1), SUB), :]
-                    tr[z, pl.ds(fy, SUB, stride=2), :] = wde * e + wny * xr[z, pl.ds(tile(t + 1) - 1, SUB), :]
-                    tr[z, pl.ds(fy + 1, SUB, stride=2), :] = wdo * e + wny * xr[z, pl.ds(tile(t + 1) + 1, SUB), :]
+                    tr[z, pl.ds(fy, SUB, stride=PAIR), :] = wde * e + wny * xr[z, pl.ds(tile(t + 1) - 1, SUB), :]
+                    tr[z, pl.ds(fy + 1, SUB, stride=PAIR), :] = wdo * e + wny * xr[z, pl.ds(tile(t + 1) + 1, SUB), :]
             loop(ncz // per, plane)
         loop(nct, ctile)
 
@@ -410,7 +436,7 @@
                 z0 = fine.zs + SUB * k
                 tb = tr[pl.ds(4 * k, 6), rows, :]
                 mid = 0.75 * tb[1:5]
-                add = jnp.stack([mid + 0.25 * tb[0:4], mid + 0.25 * tb[2:6]], axis=1).reshape(SUB, SUB, LN)
+                add = jnp.stack([mid + 0.25 * tb[0:4], mid + 0.25 * tb[PAIR:6]], axis=1).reshape(SUB, SUB, LN)
                 if fine.idx:
                     dst[pl.ds(z0, SUB), rows, :] = dst[pl.ds(z0, SUB), rows, :] + add
                     continue
@@ -426,42 +452,62 @@
                 send(dst, 0, t)
         loop(fine.nyt, ytile)
 
-    def exchange_wide(lev, ref, sendp, recvp, k):
-        n, h = lev.n, HALO_PLANES[lev.idx]
-        cx = remote(sendp, recvp, k, 1)
+    def exchange_wide(lev, ref, sendp, recvp, sendh, recvh):
+        n, h, k = lev.n, HALO_PLANES[lev.idx], lev.idx
+        hy = pl.multiple_of(jnp.where(py == 0, lev.oy + n, lev.oy - SUB), SUB)
+        hz = jnp.where(pz == 0, lev.oz + n, lev.oz - h)
+        cx = remote(sendp, recvp, 4 * k + 1, 1)
         cx.start()
-        cx.wait()
+        for copy in edge_pieces(lev, ref, 0)[1:]:
+            copy.wait()
+        loop(n // SUB, lambda j: edge_pieces(lev, ref, j)[0].wait())
+        group = lane // SUB
+        face = jnp.where(low_x, lev.ox + n - SUB, lev.ox)
         halo = jnp.where(low_x, lev.ox + n, lev.ox - SUB)
         inh = (lane >= halo) & (lane < halo + SUB)
 
+        def spots(q):
+            return pl.ds(pl.multiple_of(jnp.where(q < n // SUB, lev.oy + SUB * q, hy), SUB), SUB)
+
+        def gather_faces(z, planes, rows):
+            pk = nil
+            for i in range(planes):
+                pk = jnp.where(group == i, pltpu.roll(ref[z + i, rows, :], (SUB * i - face) & BACK, 1), pk)
+            return pk
+        nq = n // GRP
+
+        def collect_y(q):
+            sendh[q] = gather_faces(lev.oz + GRP * q, GRP, pl.ds(hy, SUB))
+
+        def collect_z(q):
+            sendh[nq + q] = gather_faces(hz, h, spots(q))
+        zper = 3 if n // SUB == SUB else n // SUB + 1
+        several(nq, PAIR, collect_y)
+        several(n // SUB + 1, zper, collect_z)
+        ch = remote(sendh, recvh, 4 * k + PAIR, 1)
+        ch.start()
+        cx.wait()
+
+        def put(pk, z, planes, rows):
+            pk = pltpu.roll(pk, halo, 1)
+            for i in range(planes):
+                ref[z + i, rows, :] = jnp.where(inh, pltpu.roll(pk, (-SUB * i) % LN, 1), ref[z + i, rows, :])
+
         def ytile(t):
             rows = pl.ds(pl.multiple_of(lev.oy + SUB * t, SUB), SUB)
-            for q in range(n // GRP):
-                pk = recvp[q, pl.ds(tile(t), SUB), :]
-                pk = pltpu.roll(pk, halo, 1)
-                for i in range(GRP):
-                    z = lev.oz + GRP * q + i
-                    ref[z, rows, :] = jnp.where(inh, pltpu.roll(pk, (-SUB * i) % LN, 1), ref[z, rows, :])
+            for q in range(nq):
+                put(recvp[q, pl.ds(tile(t), SUB), :], lev.oz + GRP * q, GRP, rows)
         loop(n // SUB, ytile)
-        fy = pl.multiple_of(jnp.where(py == 0, lev.oy + n - SUB, lev.oy), SUB)
-        hy = pl.multiple_of(jnp.where(py == 0, lev.oy - SUB, lev.oy + n), SUB)
-        fz = jnp.where(pz == 0, lev.oz + n - h, lev.oz)
-        hz = jnp.where(pz == 0, lev.oz - h, lev.oz + n)
-        copies = [
-            remote(ref.at[pl.ds(lev.oz, n), pl.ds(fy, SUB), :], ref.at[pl.ds(lev.oz, n), pl.ds(hy, SUB), :], k + 1, 2),
-            remote(ref.at[pl.ds(fz, h), pl.ds(lev.oy, n), :], ref.at[pl.ds(hz, h), pl.ds(lev.oy, n), :], k + 2, 4),
-            remote(ref.at[pl.ds(fz, h), pl.ds(fy, SUB), :], ref.at[pl.ds(hz, h), pl.ds(hy, SUB), :], k + 3, 6),
-        ]
-        for c in copies:
-            c.start()
-        for c in copies:
-            c.wait()
+        ch.wait()
+
+        several(nq, PAIR, lambda q: put(recvh[q], lev.oz + GRP * q, GRP, pl.ds(hy, SUB)))
+        several(n // SUB + 1, zper, lambda q: put(recvh[nq + q], hz, h, spots(q)))
         zghost(lev, ref)
 
-    me = 4 * pz + 2 * py + px
+    me = 4 * pz + PAIR * py + px
 
     def gather3():
-        copies = [remote(g3.at[me], g3.at[me], 14 + code, code) for code in range(1, SUB)]
+        copies = [remote(g3.at[me], g3.at[me], 13 + code, code) for code in range(1, SUB)]
         for c in copies:
             c.start()
         for c in copies:
@@ -472,11 +518,11 @@
 
         def ytile(t):
             rows = pl.ds(pl.multiple_of(lev.oy + SUB * t, SUB), SUB)
-            by = t // 2
-            r0 = pl.ds(tile(t % 2), SUB)
+            by = t // PAIR
+            r0 = pl.ds(tile(t % PAIR), SUB)
             for q in range(4):
-                lo = g3[4 * (q // 2) + 2 * by, q % 2, r0, :]
-                hi = g3[4 * (q // 2) + 2 * by + 1, q % 2, r0, :]
+                lo = g3[4 * (q // PAIR) + PAIR * by, q % PAIR, r0, :]
+                hi = g3[4 * (q // PAIR) + PAIR * by + 1, q % PAIR, r0, :]
                 for i in range(SUB):
                     a = pltpu.roll(lo, (lev.ox - GRP * i) % LN, 1)
                     b = pltpu.roll(hi, (lev.ox + GRP - GRP * i) % LN, 1)
@@ -499,8 +545,8 @@
         lines = [jnp.broadcast_to(jnp.sum(a, axis=0, keepdims=True), (SUB, LN)) for a in acc]
         own = (lane >= lev.ox) & (lane < lev.ox + SUB)
         for z in range(SUB):
-            idx = jnp.clip((z % 2) * 64 + row * SUB + lane - lev.ox, 0, 127)
-            e5[lev.oz + z, pl.ds(lev.oy, SUB), :] = jnp.where(own, jnp.take_along_axis(lines[z // 2], idx, axis=1), 0.0)
+            idx = jnp.clip((z % PAIR) * 64 + row * SUB + lane - lev.ox, 0, 127)
+            e5[lev.oz + z, pl.ds(lev.oy, SUB), :] = jnp.where(own, jnp.take_along_axis(lines[z // PAIR], idx, axis=1), 0.0)
         zghost(lev, e5)
 
     def base_of(lev):
@@ -512,27 +558,27 @@
         residual_pass(fine, v.at[0], rhs)
         descend()
         prolong_add(fine, coarse, ecoarse, v.at[0], cbase)
-        loop(2, lambda i: sweep(fine, v.at[i], v.at[1 - i], rhs))
+        loop(PAIR, lambda i: sweep(fine, v.at[i], v.at[1 - i], rhs))
 
     def descend4():
-        restrict_to(levels[4], levels[5], b5, None)
+        restrict_to(levels[4], levels[5], b5)
         coarse_solve()
 
     def descend3():
-        restrict_to(levels[3], levels[4], b4, None)
+        restrict_to(levels[3], levels[4], b4)
         zghost(levels[4], b4)
         local_visit(levels[4], v4, b4, descend4, e5, levels[5], base_of(levels[5]))
 
     def descend2():
-        restrict_packed(levels[2], me)
+        restrict_packed(levels[PAIR], me)
         gather3()
         local_visit(levels[3], v3, b3, descend3, v4.at[0], levels[4], base_of(levels[4]))
 
     def descend1():
-        restrict_to(levels[1], levels[2], b2, p2s)
-        exchange_wide(levels[2], b2, p2s, p2r, 10)
+        restrict_to(levels[1], levels[PAIR], b2, p2s)
+        exchange_wide(levels[PAIR], b2, p2s, p2r, h2s, h2r)
         oz, oy, ox = base_of(levels[3])
-        local_visit(levels[2], v2, b2, descend2, v3.at[0], levels[3], (oz + GRP * pz, oy + GRP * py, ox + GRP * px))
+        local_visit(levels[PAIR], v2, b2, descend2, v3.at[0], levels[3], (oz + GRP * pz, oy + GRP * py, ox + GRP * px))
 
     def skew_in(t):
         o = order(t)
@@ -554,15 +600,15 @@
     def correct():
         residual0()
         restrict_to(lev0, levels[1], b1, p1s)
-        exchange_wide(levels[1], b1, p1s, p1r, 6)
-        local_visit(levels[1], v1, b1, descend1, v2.at[0], levels[2], base_of(levels[2]))
+        exchange_wide(levels[1], b1, p1s, p1r, h1s, h1r)
+        local_visit(levels[1], v1, b1, descend1, v2.at[0], levels[PAIR], base_of(levels[PAIR]))
         prolong_add(lev0, levels[1], v1.at[0], ua, base_of(levels[1]))
 
     def half_cycle(h):
         sweep0(ua, ub, 0)
         sweep0(ub, ua, 1)
-        pl.when(h % 2 == 0)(correct)
-    loop(2 * CYCLES, half_cycle)
+        pl.when(h % PAIR == 0)(correct)
+    loop(PAIR * CYCLES, half_cycle)
     loop(GRP, lambda t: receive(ua, 0, t))
 
     def store(t):
@@ -586,12 +632,13 @@
 
     scratch = [vmem(130, 144, LN), vmem(130, 144, LN), vmem(LN, LN, LN), vmem(66, 144, LN), vmem(66, 80, LN), vmem(LN, SUB, LN), vmem(LN, SUB, LN)]
     for shape in ((82, 96), (50, 64), (34, 72), (18, 48)):
-        scratch += [vmem(2, *shape, LN), vmem(*shape, LN)]
+        scratch += [vmem(PAIR, *shape, LN), vmem(*shape, LN)]
     scratch += [vmem(10, 32, LN), vmem(10, 32, LN), vmem(4, 512, LN)]
-    scratch += [vmem(2, LN, LN)] * 4
-    scratch += [vmem(4, 64, LN)] * 2 + [vmem(2, 32, LN)] * 2 + [vmem(SUB, 2, GRP, LN)]
+    scratch += [vmem(PAIR, LN, LN)] * 4
+    scratch += [vmem(4, 64, LN)] * PAIR + [vmem(PAIR, 32, LN)] * PAIR
+    scratch += [vmem(13, SUB, LN)] * PAIR + [vmem(7, SUB, LN)] * PAIR + [vmem(SUB, PAIR, GRP, LN)]
     scratch += [pltpu.SemaphoreType.DMA((22,)), pltpu.SemaphoreType.DMA((22,))]
-    scratch += [pltpu.SemaphoreType.DMA((2, GRP))] * 4 + [pltpu.SemaphoreType.DMA((36,))]
+    scratch += [pltpu.SemaphoreType.DMA((PAIR, GRP))] * 6 + [pltpu.SemaphoreType.DMA((36,))]
 
     call = pl.pallas_call(
         solve_kernel,

time: 252 us -> 241 us (0.956)
  Pallas kernels: 244 us -> 233 us
    pallas_call x1, Pallas kernels: 244 us -> 233 us
where the time goes in v5:
time: 241 us
  Pallas kernels  233 us (97%)
  local copies, waits for them, and re-layouts  7.89 us (3%)
    pallas_call x1, Pallas kernels  233 us
    unnamed x1, local copies, waits for them, and re-layouts  7.89 us

profile of v5, /device:TPU:0, one launch (start us, length us, event | category | flops | bytes accessed | tf_op | source)
XLA Modules:
  0.0 240.9 jit_solution(16568080796825315611)
XLA Ops:
  0.0 233.0 %multigrid.1 = f32[128,128,128]{2,1,0:T(8,128)} custom-call(f32[128,128,128]{2,1,0:T(8,128)} %f_hbm.1, f32[128,128,128]{2,1,0:T(8,128)} %u_hbm.1, f32[512,512]{1,0:T(8,128)} %c_hbm.1), custom_call_target="tpu_custom_call" | custom-call | tf_op jit(solution)/shard_map/multigrid/pallas_call
  233.0 7.9 %copy.5 = f32[128,128,128]{2,1,0:T(8,128)} copy(f32[128,128,128]{2,1,0:T(8,128)} %multigrid.1) | data formatting | bytes 16777216

commit v6 on v5

--- a/solution.py
+++ b/solution.py
@@ -39,7 +39,7 @@
 
 
 def solve_kernel(f_hbm, u_hbm, c_hbm, out_hbm,
-                 ua, ub, fr, tr, xr, sx, sy, v1, b1, v2, b2, v3, b3, v4, b4, e5, b5, cinv,
+                 ua, ub, fr, tr, xr, sx, sy, v1, w1, b1, v2, w2, b2, v3, w3, b3, v4, w4, b4, e5, b5, cinv,
                  xs, xg, yp, yg, p1s, p1r, p2s, p2r, h1s, h1r, h2s, h2r, g3, ssem, rsem, xss, xrs, zss, zrs, wss, wrs, lsem):
     pz, py, px = lax.axis_index('gz'), lax.axis_index('gy'), lax.axis_index('gx')
     pos = (pz, py, px)
@@ -100,7 +100,7 @@
             ref[i] = jnp.zeros(ref.shape[1:], F32)
         loop(ref.shape[0], body)
 
-    for ref in (v1.at[0], v1.at[1], b1, v2.at[0], v2.at[1], b2, v3.at[0], v3.at[1], b3, v4.at[0], v4.at[1], b4, e5):
+    for ref in (v1, w1, b1, v2, w2, b2, v3, w3, b3, v4, w4, b4, e5):
         zero(ref)
 
     def zero_rows(i):
@@ -141,54 +141,71 @@
                 body(i * per + k)
         loop(count // per, step)
 
-    def roll_sums(src, zs, nzb, y0):
+    def roll_sums(src, zs, nzb, y0, sx):
         for k in range(nzb):
             c = src[pl.ds(zs + SUB * k, SUB), pl.ds(y0, SUB), :]
             sx[pl.ds(SUB * k, SUB)] = pltpu.roll(c, 1, PAIR) + pltpu.roll(c, BACK, PAIR)
 
-    def stencil(src, zs, k, y0):
+    def stencil(src, zs, k, y0, sx):
         z0 = zs + SUB * k
         v = src[pl.ds(z0 - 1, SUB + PAIR), pl.ds(y0, SUB), :]
         s = v[0:SUB] + v[PAIR:SUB + PAIR]
         s = s + src[pl.ds(z0, SUB), pl.ds(y0 - 1, SUB), :] + src[pl.ds(z0, SUB), pl.ds(y0 + 1, SUB), :]
         return v[1:SUB + 1], s + sx[pl.ds(SUB * k, SUB)]
 
+    def tiles(lev, src, span, count, body):
+        ys, zs, nzb = span
+
+        def at(t):
+            return pl.multiple_of(ys + SUB * t, SUB)
+        if lev.idx != 1:
+            def alone(t):
+                roll_sums(src, zs, nzb, at(t), sx)
+                body(at(t), lambda block: several(nzb, PAIR if nzb == 4 else 1, block), sx)
+            loop(count, alone)
+            return
+        roll_sums(src, zs, nzb, at(0), sx)
+
+        def step(t):
+            def both(now, later):
+                roll_sums(src, zs, nzb, at(t + 1 - (t + 1) // count), later)
+                body(at(t), lambda block: [block(k) for k in range(nzb)], now)
+            pl.when(t % PAIR == 0)(lambda: both(sx, sy))
+            pl.when(t % PAIR == 1)(lambda: both(sy, sx))
+        loop(count, step)
+
     def sweep(lev, src, dst, rhs):
         first = rhs is None
 
-        def ytile(t):
-            y0 = pl.multiple_of(lev.ys + SUB * t, SUB)
+        def body(y0, each, sums):
             inside, nb = coefs(lev, y0)
             cc = (1.0 - OMEGA) - C6 * nb
             if first:
                 ca, cb = jnp.where(inside, C6 * (cc + 1.0), 0.0), jnp.where(inside, C6 * C6, 0.0)
             else:
                 ca, cb = jnp.where(inside, cc, 0.0), jnp.where(inside, C6, 0.0)
-            roll_sums(src, lev.zs, lev.nzb, y0)
 
             def block(k):
-                c, s = stencil(src, lev.zs, k, y0)
+                c, s = stencil(src, lev.zs, k, y0, sums)
                 z0 = lev.zs + SUB * k
                 if not first:
                     s = s + rhs[pl.ds(z0, SUB), pl.ds(y0, SUB), :]
                 dst[pl.ds(z0, SUB), pl.ds(y0, SUB), :] = ca * c + cb * s
-            several(lev.nzb, 3 if lev.nzb == 9 else PAIR if lev.nzb == 4 else 1, block)
+            each(block)
             zghost_tile(lev, dst, y0)
-        loop(lev.nyt, ytile)
+        tiles(lev, src, (lev.ys, lev.zs, lev.nzb), lev.nyt, body)
 
     def residual_pass(lev, src, rhs):
-        def ytile(t):
-            y0 = pl.multiple_of(lev.oy + SUB * t, SUB)
+        def body(y0, each, sums):
             _, nb = coefs(lev, y0)
             dd = 6.0 + nb
-            roll_sums(src, lev.oz, lev.n // SUB, y0)
 
             def block(k):
-                c, s = stencil(src, lev.oz, k, y0)
+                c, s = stencil(src, lev.oz, k, y0, sums)
                 r = (rhs[pl.ds(lev.oz + SUB * k, SUB), pl.ds(y0, SUB), :] + (s - dd * c)).reshape(4, PAIR, SUB, LN)
-                tr[pl.ds(4 * k, 4), pl.ds(tile(t), SUB), :] = r[:, 0] + r[:, 1]
-            several(lev.n // SUB, max(1, lev.n // GRP // PAIR), block)
-        loop(lev.n // SUB, ytile)
+                tr[pl.ds(4 * k, 4), pl.ds(pl.multiple_of(y0 - lev.oy, SUB), SUB), :] = r[:, 0] + r[:, 1]
+            each(block)
+        tiles(lev, src, (lev.oy, lev.oz, lev.n // SUB), lev.n // SUB, body)
 
     zface = jnp.where(pz == 0, LN, 1)
     zdst = LN + 1 - zface + jnp.where(pz == 0, -1, 1)
@@ -552,13 +569,14 @@
     def base_of(lev):
         return (lev.oz, lev.oy, lev.ox)
 
-    def local_visit(fine, v, rhs, descend, ecoarse, coarse, cbase):
-        sweep(fine, rhs, v.at[0], None)
-        zghost(fine, v.at[0])
-        residual_pass(fine, v.at[0], rhs)
+    def local_visit(fine, v, w, rhs, descend, ecoarse, coarse, cbase):
+        sweep(fine, rhs, v, None)
+        zghost(fine, v)
+        residual_pass(fine, v, rhs)
         descend()
-        prolong_add(fine, coarse, ecoarse, v.at[0], cbase)
-        loop(PAIR, lambda i: sweep(fine, v.at[i], v.at[1 - i], rhs))
+        prolong_add(fine, coarse, ecoarse, v, cbase)
+        sweep(fine, v, w, rhs)
+        sweep(fine, w, v, rhs)
 
     def descend4():
         restrict_to(levels[4], levels[5], b5)
@@ -567,18 +585,18 @@
     def descend3():
         restrict_to(levels[3], levels[4], b4)
         zghost(levels[4], b4)
-        local_visit(levels[4], v4, b4, descend4, e5, levels[5], base_of(levels[5]))
+        local_visit(levels[4], v4, w4, b4, descend4, e5, levels[5], base_of(levels[5]))
 
     def descend2():
         restrict_packed(levels[PAIR], me)
         gather3()
-        local_visit(levels[3], v3, b3, descend3, v4.at[0], levels[4], base_of(levels[4]))
+        local_visit(levels[3], v3, w3, b3, descend3, v4, levels[4], base_of(levels[4]))
 
     def descend1():
         restrict_to(levels[1], levels[PAIR], b2, p2s)
         exchange_wide(levels[PAIR], b2, p2s, p2r, h2s, h2r)
         oz, oy, ox = base_of(levels[3])
-        local_visit(levels[PAIR], v2, b2, descend2, v3.at[0], levels[3], (oz + GRP * pz, oy + GRP * py, ox + GRP * px))
+        local_visit(levels[PAIR], v2, w2, b2, descend2, v3, levels[3], (oz + GRP * pz, oy + GRP * py, ox + GRP * px))
 
     def skew_in(t):
         o = order(t)
@@ -601,15 +619,14 @@
         residual0()
         restrict_to(lev0, levels[1], b1, p1s)
         exchange_wide(levels[1], b1, p1s, p1r, h1s, h1r)
-        local_visit(levels[1], v1, b1, descend1, v2.at[0], levels[PAIR], base_of(levels[PAIR]))
-        prolong_add(lev0, levels[1], v1.at[0], ua, base_of(levels[1]))
+        local_visit(levels[1], v1, w1, b1, descend1, v2, levels[PAIR], base_of(levels[PAIR]))
+        prolong_add(lev0, levels[1], v1, ua, base_of(levels[1]))
 
     def half_cycle(h):
         sweep0(ua, ub, 0)
         sweep0(ub, ua, 1)
         pl.when(h % PAIR == 0)(correct)
     loop(PAIR * CYCLES, half_cycle)
-    loop(GRP, lambda t: receive(ua, 0, t))
 
     def store(t):
         return pltpu.make_async_copy(ub.at[pl.ds(1, LN), pl.ds(tile(t + 1), SUB), :], out_hbm.at[:, pl.ds(tile(t), SUB), :],
@@ -621,6 +638,7 @@
             ub[z + 1, rows, :] = pltpu.roll(ua[z + 1, rows, :], -z % LN, 1)
         store(t).start()
     loop(GRP, skew_out)
+    loop(GRP, lambda t: receive(ua, 0, t))
     loop(GRP, lambda t: store(t).wait())
 
 
@@ -632,7 +650,7 @@
 
     scratch = [vmem(130, 144, LN), vmem(130, 144, LN), vmem(LN, LN, LN), vmem(66, 144, LN), vmem(66, 80, LN), vmem(LN, SUB, LN), vmem(LN, SUB, LN)]
     for shape in ((82, 96), (50, 64), (34, 72), (18, 48)):
-        scratch += [vmem(PAIR, *shape, LN), vmem(*shape, LN)]
+        scratch += [vmem(*shape, LN)] * 3
     scratch += [vmem(10, 32, LN), vmem(10, 32, LN), vmem(4, 512, LN)]
     scratch += [vmem(PAIR, LN, LN)] * 4
     scratch += [vmem(4, 64, LN)] * PAIR + [vmem(PAIR, 32, LN)] * PAIR

time: 241 us -> 236 us (0.979)
  Pallas kernels: 233 us -> 228 us
    pallas_call x1, Pallas kernels: 233 us -> 228 us
where the time goes in v6:
time: 236 us; the launch traced here: 235 us
  Pallas kernels  228 us (97%)
  local copies, waits for them, and re-layouts  7.89 us (3%)
    pallas_call x1, Pallas kernels  228 us
    unnamed x1, local copies, waits for them, and re-layouts  7.89 us

profile of v6, /device:TPU:0, one launch (start us, length us, event | category | flops | bytes accessed | tf_op | source)
XLA Modules:
  0.0 235.4 jit_solution(12792998918242803446)
XLA Ops:
  0.0 227.5 %multigrid.1 = f32[128,128,128]{2,1,0:T(8,128)} custom-call(f32[128,128,128]{2,1,0:T(8,128)} %f_hbm.1, f32[128,128,128]{2,1,0:T(8,128)} %u_hbm.1, f32[512,512]{1,0:T(8,128)} %c_hbm.1), custom_call_target="tpu_custom_call" | custom-call | tf_op jit(solution)/shard_map/multigrid/pallas_call
  227.5 7.9 %copy.5 = f32[128,128,128]{2,1,0:T(8,128)} copy(f32[128,128,128]{2,1,0:T(8,128)} %multigrid.1) | data formatting | bytes 16777216

commit v7 on v6

--- a/solution.py
+++ b/solution.py
@@ -79,6 +79,12 @@
     def loop(n, body):
         lax.fori_loop(0, n, lambda i, c: (body(i), c)[1], 0)
 
+    def several(count, per, body):
+        def step(i):
+            for k in range(per):
+                body(i * per + k)
+        loop(count // per, step)
+
     def tile(i):
         return pl.multiple_of(SUB * i, SUB)
 
@@ -98,7 +104,7 @@
     def zero(ref):
         def body(i):
             ref[i] = jnp.zeros(ref.shape[1:], F32)
-        loop(ref.shape[0], body)
+        several(ref.shape[0], PAIR, body)
 
     for ref in (v1, w1, b1, v2, w2, b2, v3, w3, b3, v4, w4, b4, e5):
         zero(ref)
@@ -135,12 +141,6 @@
     def zghost(lev, ref):
         loop(lev.shape[1] // SUB, lambda t: zghost_tile(lev, ref, tile(t)))
 
-    def several(count, per, body):
-        def step(i):
-            for k in range(per):
-                body(i * per + k)
-        loop(count // per, step)
-
     def roll_sums(src, zs, nzb, y0, sx):
         for k in range(nzb):
             c = src[pl.ds(zs + SUB * k, SUB), pl.ds(y0, SUB), :]
@@ -158,7 +158,7 @@
 
         def at(t):
             return pl.multiple_of(ys + SUB * t, SUB)
-        if lev.idx != 1:
+        if lev.idx > PAIR:
             def alone(t):
                 roll_sums(src, zs, nzb, at(t), sx)
                 body(at(t), lambda block: several(nzb, PAIR if nzb == 4 else 1, block), sx)

time: 236 us -> 233 us (0.987)
  Pallas kernels: 228 us -> 225 us
    pallas_call x1, Pallas kernels: 228 us -> 225 us
where the time goes in v7:
time: 233 us
  Pallas kernels  225 us (97%)
  local copies, waits for them, and re-layouts  7.89 us (3%)
    pallas_call x1, Pallas kernels  225 us
    unnamed x1, local copies, waits for them, and re-layouts  7.89 us

profile of v7, /device:TPU:0, one launch (start us, length us, event | category | flops | bytes accessed | tf_op | source)
XLA Modules:
  0.0 232.9 jit_solution(11683112556241925144)
XLA Ops:
  0.0 225.0 %multigrid.1 = f32[128,128,128]{2,1,0:T(8,128)} custom-call(f32[128,128,128]{2,1,0:T(8,128)} %f_hbm.1, f32[128,128,128]{2,1,0:T(8,128)} %u_hbm.1, f32[512,512]{1,0:T(8,128)} %c_hbm.1), custom_call_target="tpu_custom_call" | custom-call | tf_op jit(solution)/shard_map/multigrid/pallas_call
  225.0 7.9 %copy.5 = f32[128,128,128]{2,1,0:T(8,128)} copy(f32[128,128,128]{2,1,0:T(8,128)} %multigrid.1) | data formatting | bytes 16777216
